TPU v7x, 256 devices: a whole 4x4x8 slice. The times are simulated.
256 devices in a mesh: rack: 8 (over x, core), chip: 32 (over y, z).
Axes of the slice: x: 4, y: 4, z: 8, core: 2. Of those that a mesh axis runs over, the one named last changes fastest.
Arguments:
- points: float32 [512, 4, 32, 256], P(('rack', 'chip')), may hold values from -6 to 6
- counts: int32 [512, 256], P(('rack', 'chip')), may hold values from 1 to 32
- cells: int32 [512, 256], P(('rack', 'chip')), may hold values from 0 to 2047, as said below
- pfn_weight: float32 [9, 64], replicated, may hold values from -2 to 2
- pfn_gain: float32 [64], replicated, may hold values from 0.5 to 1.5
- pfn_bias: float32 [64], replicated, may hold values from -3 to 3
- conv_weight: float32 [4, 9, 4096], replicated, may hold values from -0.25 to 0.25
- bn_gain: float32 [4, 64], replicated, may hold values from 0.5 to 1.5
- bn_bias: float32 [4, 64], replicated, may hold values from -3 to 3
- cotangent: float32 [512, 64, 4, 128], P(('rack', 'chip')), may hold values from -0.006 to 0.006
Outputs:
- features: float32 [512, 64, 4, 128], P(('rack', 'chip'))
- conv_grads: float32 [4, 9, 4096], replicated
- norm_grads: float32 [2, 4, 64], replicated
- pillar_grad: float32 [512, 64, 256], P(('rack', 'chip'))
Inputs may be any that keep to these rules, and one draw needn't show every extreme that they name: `cells`: within one sweep no two pillars share a cell.
All inputs are finite; a program needn't handle non-finite values.
Results may differ from a plain program's by a relative error of at most 0.0003.
Values sent between devices are 32-bit elements; how exact they have to be, the bound alone decides.
No kernel may reach another device: no remote copies, remote signals or barrier semaphores. Data moves between devices by JAX's collectives and lax.ppermute only.
A program may use at most 128 MiB of HBM per device.

v0:
```python
import functools

import jax
import jax.numpy as jnp
from jax import lax
from jax.experimental import pallas as pl
from jax.experimental.pallas import tpu as pltpu
from jax.sharding import Mesh
from jax.sharding import PartitionSpec as P

C = 64
MAXP = 32
LAYERS = 4
GH = 8
GW = 256
PILL = 256
NS = 2
TAP_ROWS = C * C // 128
BLOCK = 4 * TAP_ROWS
OH = GH // 2
OW = GW // 2
POS = OH * OW
NPOS = NS * POS
PADW = (OH + 2) * OW
EPS = 1e-05
F32 = jnp.float32
BF16 = jnp.bfloat16
ALL = ("x", "k", "y", "z")
WIDE = ("x", "y", "z")
INTERPRET = False


def split(v):
    hi = v.astype(BF16)
    return hi, (v - hi.astype(F32)).astype(BF16)


def dot_nn(a, b):
    return lax.dot_general(a, b, (((1,), (0,)), ((), ())), preferred_element_type=F32)


def dot_nt(a, b):
    return lax.dot_general(a, b, (((1,), (1,)), ((), ())), preferred_element_type=F32)


def dot3(dot, a_hi, a_lo, b_hi, b_lo):
    m = a_hi.shape[0]
    both = dot(jnp.concatenate([a_hi, a_lo], axis=0), b_hi)
    return both[:m] + both[m:] + dot(a_hi, b_lo)


def columns(row):
    return jnp.transpose(jnp.broadcast_to(row, (128, 128)))


def to_row(top, bottom):
    return jnp.sum(jnp.transpose(jnp.concatenate([top, bottom], axis=0)), axis=0, keepdims=True)


def lanes128():
    return lax.broadcasted_iota(jnp.int32, (C, 128), 1)


def from_left(v, lane):
    return jnp.where(lane == 0, 0.0, pltpu.roll(v, 1, 1))


def from_right(v, lane):
    return jnp.where(lane == 127, 0.0, pltpu.roll(v, 127, 1))


def lanes_from(start, size=OW):
    return pl.ds(pl.multiple_of(start, 128), size)


def each_sweep(body, init=0):
    return lax.fori_loop(0, NS, body, init)


def each_row(body):
    def step(t, _):
        n = lax.div(t, OH)
        body(lanes_from(t * OW), n, t - n * OH)
        return _

    lax.fori_loop(0, NS * OH, step, 0)


def put(hi_ref, lo_ref, row, col, v):
    hi, lo = split(v)
    col = pl.multiple_of(col, 128)
    hi_ref[pl.ds(row, C), pl.ds(col, 128)] = hi
    lo_ref[pl.ds(row, C), pl.ds(col, 128)] = lo


def put_shifted(hi_ref, lo_ref, n, r, v, lane):
    col = n * PADW + (r + 1) * OW
    put(hi_ref, lo_ref, 0, col, from_left(v, lane))
    put(hi_ref, lo_ref, C, col, v)
    put(hi_ref, lo_ref, 2 * C, col, from_right(v, lane))


def zero_borders(refs):
    for ref in refs:
        for n in range(NS):
            for r in (0, OH + 1):
                ref[:, pl.ds(n * PADW + r * OW, OW)] = jnp.zeros((3 * C, OW), BF16)


def conv_padded(w_hi, w_lo, hi_ref, lo_ref, n):
    cols = lanes_from(n * PADW, PADW)
    p = dot3(dot_nn, w_hi, w_lo, hi_ref[:, cols], lo_ref[:, cols])
    return p[:C, :POS] + p[C : 2 * C, OW : OW + POS] + p[2 * C :, 2 * OW : 2 * OW + POS]


def choose(layer, layers, read):
    value = read(layers[0])
    for l in layers[1:]:
        value = jnp.where(layer == l, read(l), value)
    return value


def tap_block(w_ref, buf_ref, layer, layers, tap):
    packed = choose(
        layer, layers, lambda l: w_ref[pl.ds(tap * TAP_ROWS * LAYERS + l, TAP_ROWS, stride=LAYERS), :]
    )
    buf_ref[pl.ds(0, TAP_ROWS, stride=2), :] = packed[:, :C]
    buf_ref[pl.ds(1, TAP_ROWS, stride=2), :] = packed[:, C:]
    return buf_ref[...]


def forward_weights(w_ref, buf_ref, layer, layers):
    rows = []
    for a in range(3):
        rows.append(jnp.concatenate([tap_block(w_ref, buf_ref, layer, layers, 3 * a + b) for b in range(3)], axis=1))
    return jnp.concatenate(rows, axis=0)


def backward_weights(w_ref, buf_ref, layer, layers):
    rows = []
    for a in range(3):
        blocks = [jnp.transpose(tap_block(w_ref, buf_ref, layer, layers, 3 * (2 - a) + 2 - b)) for b in range(3)]
        rows.append(jnp.concatenate(blocks, axis=1))
    return jnp.concatenate(rows, axis=0)


def first_backward_weights(w_ref, buf_ref):
    rows = []
    for a in range(3):
        left, mid, right = (jnp.transpose(tap_block(w_ref, buf_ref, 0, (0,), 3 * a + b)) for b in range(3))
        rows.append(jnp.concatenate([mid, jnp.zeros((C, C), F32)], axis=1))
        rows.append(jnp.concatenate([right, left], axis=1))
    return jnp.concatenate(rows, axis=0)


def gain_bias(gain_ref, bias_ref, layer, layers):
    def row(l):
        at = pl.ds(l, 1)
        return jnp.concatenate([gain_ref[at, :], bias_ref[at, :]], axis=1)

    gb = columns(choose(layer, layers, row))
    return gb[:C], gb[C:]


def first_core():
    return lax.axis_index("k") == 0


def store_half(refs, slot, mine_first, mine_second):
    keep_ref, send_ref = refs
    first = first_core()
    for t in range(4):
        at = pl.ds(8 + slot * BLOCK + t * TAP_ROWS, TAP_ROWS)
        keep_ref[at, :] = jnp.where(first, mine_first[t], mine_second[t])
        send_ref[at, :] = jnp.where(first, mine_second[t], mine_first[t])


def store_kernel_grad(refs, slot, per_row, buf_ref):
    def packed(tap):
        a, b = divmod(tap, 3)
        buf_ref[...] = per_row[a][:, b * C : (b + 1) * C]
        even = buf_ref[pl.ds(0, TAP_ROWS, stride=2), :]
        odd = buf_ref[pl.ds(1, TAP_ROWS, stride=2), :]
        return jnp.concatenate([even, odd], axis=1)

    taps = [packed(tap) for tap in range(9)]
    store_half(refs, slot, taps[:4], taps[4:8])
    return taps[8]


def rows_of(g_ref, stride, index):
    peers = g_ref.shape[0] // stride
    if stride == 1:
        return g_ref[...]
    return g_ref[pl.ds(index, peers, stride=stride), :]


def reduced_rows(g_ref, stride, red_ref, count):
    for j in range(count):
        red_ref[pl.ds(j, 1), :] = jnp.sum(rows_of(g_ref, stride, 1 + j), axis=0, keepdims=True)


def store_stats(z_ref, part_ref):
    acc = z_ref[:, pl.ds(0, 128)]
    for t in range(1, NPOS // 128):
        acc = acc + z_ref[:, pl.ds(t * 128, 128)]
    mean = jnp.sum(acc, axis=1, keepdims=True) * (1.0 / NPOS)
    sq = jnp.zeros((C, 128), F32)
    for t in range(NPOS // 128):
        d = z_ref[:, pl.ds(t * 128, 128)] - mean
        sq = sq + d * d
    lane = lax.broadcasted_iota(jnp.int32, (1, 128), 1)
    part_ref[pl.ds(0, 1), :] = to_row(acc, sq) * jnp.where(lane < C, 1.0 / NPOS, 1.0)


def gathered_stats(g):
    rows = g.shape[0]
    total = jnp.sum(g, axis=0, keepdims=True)
    mean = total * (1.0 / rows)
    dev = g - mean
    spread = jnp.sum(dev * dev, axis=0, keepdims=True)
    each = 2.0 * NPOS
    var = (total + each * pltpu.roll(jnp.broadcast_to(spread, (8, 128)), C, 1)[:1]) * (1.0 / (each * rows))
    lane = lax.broadcasted_iota(jnp.int32, (1, 128), 1)
    return jnp.where(lane < C, mean, lax.rsqrt(var + EPS))


def pfn_kernel(pts_in, cnt_in, cell_in, w_in, hmax_ref, part_ref, base_ref, w_pad, pts_ref, cnt_ref, cell_ref, w_ref, sems):
    copies = [
        pltpu.make_async_copy(src, dst, sems.at[i])
        for i, (src, dst) in enumerate(
            ((pts_in, pts_ref), (cnt_in, cnt_ref), (cell_in, cell_ref), (w_in, w_ref))
        )
    ]
    for copy in copies:
        copy.start()
    for copy in copies:
        copy.wait()
    w_pad[...] = jnp.zeros((128, 128), F32)
    w_pad[pl.ds(0, 9), pl.ds(0, C)] = w_ref[...]
    w_cols = jnp.transpose(w_pad[...])

    def col(j):
        return w_cols[:C, j : j + 1]

    wx = col(0) + col(4) + col(7)
    wy = col(1) + col(5) + col(8)
    wz = col(2) + col(6)
    wr = col(3)
    slot = lax.broadcasted_iota(jnp.int32, (MAXP, PILL), 0)
    total = jnp.zeros((C, 1), F32)
    number = jnp.zeros((1, 1), F32)
    for n in range(NS):
        count_i = cnt_ref[pl.ds(n, 1), :]
        count = count_i.astype(F32)
        valid = slot < count_i
        sums = []
        for j in range(4):
            p = pts_ref[pl.ds((n * 4 + j) * MAXP, MAXP), :]
            sums.append(jnp.sum(jnp.where(valid, p, 0.0), axis=0, keepdims=True))
        cell = cell_ref[pl.ds(n, 1), :]
        col_pos = jnp.bitwise_and(cell, GW - 1).astype(F32) * (2.0 / GW) - 1.0
        row_pos = jnp.right_shift(cell, 8).astype(F32) * (2.0 / GH) - 1.0
        base = -(
            col(4) * (sums[0] / count)
            + col(5) * (sums[1] / count)
            + col(6) * (sums[2] / count)
            + col(7) * col_pos
            + col(8) * row_pos
        )
        base_ref[:, pl.ds(n * PILL, PILL)] = base
        weighted = wx * sums[0] + wy * sums[1] + wz * sums[2] + wr * sums[3] + base * count
        total = total + jnp.sum(weighted, axis=1, keepdims=True)
        number = number + jnp.sum(count, axis=1, keepdims=True)
    mean = total / number
    sq_parts = []
    half = C // 2
    for c0 in (0, half):
        ch = slice(c0, c0 + half)
        bx = jnp.broadcast_to(wx[ch], (half, 128))
        by = jnp.broadcast_to(wy[ch], (half, 128))
        bz = jnp.broadcast_to(wz[ch], (half, 128))
        br = jnp.broadcast_to(wr[ch], (half, 128))
        mb = jnp.broadcast_to(mean[ch], (half, 128))
        sq = jnp.zeros((half, 128), F32)
        for n in range(NS):
            for q in range(PILL // 128):
                lanes = pl.ds(q * 128, 128)
                base = base_ref[pl.ds(c0, half), pl.ds(n * PILL + q * 128, 128)] - mb
                count = cnt_ref[pl.ds(n, 1), lanes]

                def step(k8, carry, n=n, lanes=lanes, base=base, count=count, bx=bx, by=by, bz=bz, br=br):
                    best, sq = carry
                    p = [
                        pts_ref[pl.ds(pl.multiple_of((n * 4 + j) * MAXP + k8 * 8, 8), 8), lanes]
                        for j in range(4)
                    ]
                    for i in range(8):
                        px, py, pz, pr = (v[i : i + 1] for v in p)
                        d = bx * px + by * py + (bz * pz + br * pr) + base
                        ok = jnp.broadcast_to(k8 * 8 + i < count, (half, 128))
                        best = jnp.where(ok, jnp.maximum(best, d), best)
                        sq = sq + jnp.where(ok, d * d, 0.0)
                    return best, sq

                start = jnp.full((half, 128), -3.0e38, F32)
                best, sq = lax.fori_loop(0, MAXP // 8, step, (start, sq))
                hmax_ref[pl.ds(c0, half), pl.ds(n * PILL + q * 128, 128)] = best + mb
        sq_parts.append(sq)
    lane = lanes128()
    part_ref[pl.ds(0, 1), :] = to_row(
        jnp.where(lane == 0, total, 0.0), jnp.concatenate(sq_parts, axis=0)
    )
    part_ref[pl.ds(1, 1), :] = jnp.broadcast_to(number, (1, 128))


def cells_of(cell_ref, n):
    return jnp.where(n == 0, cell_ref[pl.ds(0, 1), :], cell_ref[pl.ds(1, 1), :])


def target_lane(cell):
    row = jnp.right_shift(cell, 8)
    col = jnp.bitwise_and(cell, GW - 1)
    phase = jnp.bitwise_and(row, 1) * 2 + jnp.bitwise_and(col, 1)
    return phase * POS + jnp.right_shift(row, 1) * OW + jnp.right_shift(col, 1)


def build_onehot(oht_ref, cell):
    target = jnp.broadcast_to(target_lane(cell), (256, PILL))
    iota = lax.broadcasted_iota(jnp.int32, (256, PILL), 0)
    for t in range(GH * GW // 256):
        oht_ref[pl.ds(t * 256, 256), :] = jnp.where(iota + t * 256 == target, 1.0, 0.0).astype(BF16)


def first_conv_kernel(
    g_ref, hmax_ref, cell_ref, gain_ref, bias_ref, w_ref,
    z_ref, part_ref, ev_hi, ev_lo, od_hi, od_lo,
    oht_ref, place_ref, buf_ref,
):
    s = rows_of(g_ref, 2, 0)
    num = rows_of(g_ref, 2, 1)
    total = jnp.sum(s, axis=0, keepdims=True)
    number = jnp.sum(num, axis=0, keepdims=True)
    mean = total / number
    dev = s / num - mean
    spread = jnp.sum(num * dev * dev, axis=0, keepdims=True)
    var = (total + pltpu.roll(jnp.broadcast_to(spread, (8, 128)), C, 1)[:1]) / number
    lane_row = lax.broadcasted_iota(jnp.int32, (1, 128), 1)
    stats = columns(jnp.where(lane_row < C, mean, lax.rsqrt(var + EPS)))
    mean_c, inv_c = stats[:C], stats[C:]
    gain, bias = gain_bias(gain_ref, bias_ref, 0, (0,))
    lane = lanes128()
    w_hi, w_lo = split(forward_weights(w_ref, buf_ref, 0, (0,)))
    outer_hi = jnp.concatenate([w_hi[:C], w_hi[2 * C :]], axis=0)
    outer_lo = jnp.concatenate([w_lo[:C], w_lo[2 * C :]], axis=0)

    def sweep(n, _):
        build_onehot(oht_ref, cells_of(cell_ref, n))
        tiles = []
        for q in range(PILL // 128):
            h = hmax_ref[:, lanes_from(n * PILL + q * 128)]
            tiles.append(jnp.maximum(gain * (h - mean_c) * inv_c + bias, 0.0))
        p_hi, p_lo = split(jnp.concatenate(tiles, axis=1))
        place_ref[...] = dot_nt(jnp.concatenate([p_hi, p_lo], axis=0), oht_ref[...])
        for pr, refs in ((0, (ev_hi, ev_lo)), (1, (od_hi, od_lo))):
            for part, ref in enumerate(refs):
                width = POS + pr * OW
                if pr:
                    ref[:, lanes_from(n * width)] = jnp.zeros((3 * C, OW), BF16)
                for r in range(OH):
                    even = place_ref[pl.ds(part * C, C), pl.ds(pr * 2 * POS + r * OW, OW)]
                    odd = place_ref[pl.ds(part * C, C), pl.ds((pr * 2 + 1) * POS + r * OW, OW)]
                    at = lanes_from(n * width + (r + pr) * OW)
                    ref[pl.ds(0, C), at] = from_left(odd, lane).astype(BF16)
                    ref[pl.ds(C, C), at] = even.astype(BF16)
                    ref[pl.ds(2 * C, C), at] = odd.astype(BF16)
        at = lanes_from(n * POS, POS)
        z = dot3(dot_nn, w_hi[C : 2 * C], w_lo[C : 2 * C], ev_hi[:, at], ev_lo[:, at])
        at = lanes_from(n * (POS + OW), POS + OW)
        p = dot3(dot_nn, outer_hi, outer_lo, od_hi[:, at], od_lo[:, at])
        z_ref[:, lanes_from(n * POS, POS)] = z + p[:C, :POS] + p[C:, OW:]
        return _

    each_sweep(sweep)
    store_stats(z_ref, part_ref)


def first_grad_rows(grad_of, grid_refs):
    ev_hi, ev_lo, od_hi, od_lo = grid_refs

    def sweep(n, rows):
        g_hi, g_lo = grad_of(n)
        out = []
        for row, hi, lo, start in zip(
            rows,
            (od_hi, ev_hi, od_hi),
            (od_lo, ev_lo, od_lo),
            (n * (POS + OW), n * POS, n * (POS + OW) + OW),
        ):
            at = lanes_from(start, POS)
            out.append(row + dot3(dot_nt, g_hi, g_lo, hi[:, at], lo[:, at]))
        return tuple(out)

    return each_sweep(sweep, tuple(jnp.zeros((C, 3 * C), F32) for _ in range(3)))


def first_input_sums(grid_refs):
    ev_hi, ev_lo, od_hi, od_lo = grid_refs
    one = jnp.ones((16, POS), BF16)

    def sweep(n, rows):
        out = []
        for row, hi, lo, start in zip(
            rows,
            (od_hi, ev_hi, od_hi),
            (od_lo, ev_lo, od_lo),
            (n * (POS + OW), n * POS, n * (POS + OW) + OW),
        ):
            at = lanes_from(start, POS)
            out.append(row + dot_nt(one, hi[:, at]) + dot_nt(one, lo[:, at]))
        return tuple(out)

    rows = each_sweep(sweep, tuple(jnp.zeros((16, 3 * C), F32) for _ in range(3)))
    return [jnp.broadcast_to(row[:1], (C, 3 * C)) for row in rows]


def conv_kernel(
    l_ref, g_ref, z_ref, gain_ref, bias_ref, w_ref, out_ref, part_ref, stats_ref, s_hi, s_lo, buf_ref
):
    layer = l_ref[0]
    stats = columns(gathered_stats(g_ref[...]))
    stats_ref[...] = stats
    mean, inv = stats[:C], stats[C:]
    gain, bias = gain_bias(gain_ref, bias_ref, layer - 1, (0, 1, 2))
    lane = lanes128()
    zero_borders((s_hi, s_lo))
    w_hi, w_lo = split(forward_weights(w_ref, buf_ref, layer, (1, 2, 3)))

    def activate(at, n, r):
        y = gain * ((z_ref[:, at] - mean) * inv) + bias
        put_shifted(s_hi, s_lo, n, r, y * jax.nn.sigmoid(y), lane)

    def sweep(n, _):
        out_ref[:, lanes_from(n * POS, POS)] = conv_padded(w_hi, w_lo, s_hi, s_lo, n)
        return _

    each_row(activate)
    each_sweep(sweep)
    store_stats(out_ref, part_ref)


def turn_kernel(
    g_ref, z_ref, gain_ref, bias_ref, ct_ref, z0_ref, stats0_ref, ev_hi, ev_lo, od_hi, od_lo,
    feat_ref, gy_ref, keep_ref, send_ref, stats_ref,
    buf_ref,
):
    stats = columns(gathered_stats(g_ref[...]))
    stats_ref[...] = stats
    mean, inv = stats[:C], stats[C:]
    gain, bias = gain_bias(gain_ref, bias_ref, LAYERS - 1, (LAYERS - 1,))
    dy = jnp.zeros((C, 128), F32)
    dx = jnp.zeros((C, 128), F32)
    for n in range(NS):
        for r in range(OH):
            at = pl.ds(n * POS + r * OW, OW)
            rows = pl.ds(n * C * OH + r, C, stride=OH)
            xhat = (z_ref[:, at] - mean) * inv
            y = gain * xhat + bias
            sg = jax.nn.sigmoid(y)
            feat_ref[rows, :] = y * sg
            gy = ct_ref[rows, :] * (sg * (1.0 + y * (1.0 - sg)))
            gy_ref[:, at] = gy
            dy = dy + gy
            dx = dx + gy * xhat
    part = to_row(dy, dx)
    keep_ref[pl.ds(0, 1), :] = part
    send_ref[pl.ds(0, 1), :] = part
    mean0, inv0 = stats0_ref[pl.ds(0, C), pl.ds(0, 1)], stats0_ref[pl.ds(C, C), pl.ds(0, 1)]
    grads = first_grad_rows(
        lambda n: split((z0_ref[:, lanes_from(n * POS, POS)] - mean0) * inv0), (ev_hi, ev_lo, od_hi, od_lo)
    )
    refs = (keep_ref, send_ref)
    none = jnp.zeros((TAP_ROWS, 128), F32)
    last = store_kernel_grad(refs, 0, grads, buf_ref)
    store_half(refs, 2, [last, none, none, none], [none] * 4)
    grads = first_input_sums((ev_hi, ev_lo, od_hi, od_lo))
    last = store_kernel_grad(refs, 1, grads, buf_ref)
    store_half(refs, 3, [last, none, none, none], [none] * 4)


def grad_scales(g, stats, gain):
    total = jnp.sum(g, axis=0, keepdims=True)
    entries = 2.0 * NPOS * g.shape[0]
    t = columns(total * (1.0 / entries))
    return gain * stats[C:], t[:C], t[C:], total


def back_kernel(
    g_ref, z_ref, gy_ref, stats_ref, gain_ref, bias_ref, zp_ref, statsp_ref, w_ref, *refs, layers, stride
):
    (layer,) = layers
    if layer == 1:
        grid0, last3_ref, last2_ref, refs = refs[:4], refs[4], refs[5], refs[6:]
    gyp_ref, keep_ref, send_ref, sums_ref, red_ref, *refs = refs
    if layer != 1:
        last_ref, *refs = refs
    s_hi, s_lo, a_hi, a_lo, slope_ref, buf_ref = refs
    reduced_rows(g_ref, stride, red_ref, red_ref.shape[0])
    stats = stats_ref[...]
    mean, inv = stats[:C], stats[C:]
    gain, _ = gain_bias(gain_ref, bias_ref, layer, layers)
    scale, mean_dy, mean_dx, sums_ref[...] = grad_scales(rows_of(g_ref, stride, 0), stats, gain)
    statsp = statsp_ref[...]
    meanp, invp = statsp[:C], statsp[C:]
    gainp, biasp = gain_bias(gain_ref, bias_ref, layer - 1, tuple(l - 1 for l in layers))
    lane = lanes128()
    zero_borders((s_hi, s_lo, a_hi, a_lo))
    w_hi, w_lo = split(backward_weights(w_ref, buf_ref, layer, layers))

    def turn_back(at, n, r):
        xhat = (z_ref[:, at] - mean) * inv
        gz = scale * (gy_ref[:, at] - mean_dy - xhat * mean_dx)
        put_shifted(s_hi, s_lo, n, r, gz, lane)
        y = gainp * ((zp_ref[:, at] - meanp) * invp) + biasp
        sg = jax.nn.sigmoid(y)
        slope_ref[:, at] = sg * (1.0 + y * (1.0 - sg))
        put_shifted(a_hi, a_lo, n, r, y * sg, lane)

    def sweep(n, carry):
        dy, dx = carry
        u = conv_padded(w_hi, w_lo, s_hi, s_lo, n)
        for r in range(OH):
            at = lanes_from(n * POS + r * OW)
            gy = u[:, r * OW : (r + 1) * OW] * slope_ref[:, at]
            gyp_ref[:, at] = gy
            dy = dy + gy
            dx = dx + gy * ((zp_ref[:, at] - meanp) * invp)
        return dy, dx

    each_row(turn_back)
    zero = jnp.zeros((C, 128), F32)
    dy, dx = each_sweep(sweep, (zero, zero))
    part = to_row(dy, dx)
    keep_ref[pl.ds(0, 1), :] = part
    send_ref[pl.ds(0, 1), :] = part
    span = NS * PADW - 2 * OW
    g_at = pl.ds(OW, span)
    g_hi, g_lo = s_hi[pl.ds(C, C), g_at], s_lo[pl.ds(C, C), g_at]
    rows = [
        dot3(dot_nt, g_hi, g_lo, a_hi[:, pl.ds(a * OW, span)], a_lo[:, pl.ds(a * OW, span)]) for a in range(3)
    ]
    refs = (keep_ref, send_ref)
    last = store_kernel_grad(refs, 0, rows, buf_ref)
    if layer == 1:
        rows = first_grad_rows(lambda n: split(gyp_ref[:, lanes_from(n * POS, POS)]), grid0)
        last0 = store_kernel_grad(refs, 1, rows, buf_ref)
        none = jnp.zeros((TAP_ROWS, 128), F32)
        store_half(refs, 2, [last0, none, none, none], [last, last2_ref[...], last3_ref[...], none])
        store_half(refs, 3, [none] * 4, [none] * 4)
    else:
        last_ref[...] = last


def pick_channels(tile, pair, lane):
    row = lax.broadcasted_iota(jnp.int32, (C, 128), 0)
    want = 2 * pair + jnp.where(lane < C, 0, 1)
    return jnp.sum(jnp.where(row == want, tile, 0.0), axis=0, keepdims=True)


def last_back_kernel(
    g_ref, z_ref, gy_ref, stats_ref, gain_ref, bias_ref, cell_ref, w_ref,
    first_red, red3, red2, sums1, sums2, sums3,
    pg_ref, norm_ref, own_ref,
    t_hi, t_lo, u_hi, oht_ref, buf_ref, *, stride,
):
    stats = stats_ref[...]
    mean, inv = stats[:C], stats[C:]
    gain, _ = gain_bias(gain_ref, bias_ref, 0, (0,))
    scale, mean_dy, mean_dx, sums0 = grad_scales(rows_of(g_ref, stride, 0), stats, gain)
    for l, row in enumerate((sums0, sums1[...], sums2[...], sums3[...])):
        norm_ref[pl.ds(l, 1), :] = row[:, C:]
        norm_ref[pl.ds(LAYERS + l, 1), :] = row[:, :C]
    lane = lanes128()
    count = red3.shape[0]
    peers = BLOCK // count
    spot = lax.axis_index(WIDE)

    def first_grad(raw, normed, plain, pair):
        return pick_channels(scale, pair, lane) * (
            raw - pick_channels(mean_dy, pair, lane) * plain - pick_channels(mean_dx, pair, lane) * normed
        )

    for j in range(count):
        pair = lax.rem(j * peers + spot, TAP_ROWS)
        here, raw, ends = (
            jnp.sum(rows_of(g_ref, stride, 1 + q * count + j), axis=0, keepdims=True) for q in range(3)
        )
        normed, plain, normed_end, plain_end = (first_red[pl.ds(q * count + j, 1), :] for q in range(4))
        ends = jnp.where(first_core(), first_grad(ends, normed_end, plain_end, pair), ends)
        own = (first_grad(raw, normed, plain, pair), here, red2[pl.ds(j, 1), :], red3[pl.ds(j, 1), :], ends)
        for q in range(5):
            own_ref[pl.ds(q * count + j, 1), :] = own[q]
    v_hi, v_lo = split(first_backward_weights(w_ref, buf_ref))

    def sweep(n, _):
        for ref in (t_hi, t_lo):
            ref[:, pl.ds(POS, OW)] = jnp.zeros((2 * C, OW), BF16)
        for r in range(OH):
            at = lanes_from(n * POS + r * OW)
            xhat = (z_ref[:, at] - mean) * inv
            gz = scale * (gy_ref[:, at] - mean_dy - xhat * mean_dx)
            put(t_hi, t_lo, 0, r * OW, gz)
            put(t_hi, t_lo, C, r * OW, from_right(gz, lane))
        v = dot3(dot_nn, v_hi, v_lo, t_hi[...], t_lo[...])
        for pc in range(2):
            above = v[pc * C : (pc + 1) * C, OW:]
            here = v[(2 + pc) * C : (3 + pc) * C, :POS]
            below = v[(4 + pc) * C : (5 + pc) * C, :POS]
            for pr, u in ((0, here), (1, below + above)):
                at = pl.ds((pr * 2 + pc) * POS, POS)
                hi, lo = split(u)
                u_hi[pl.ds(0, C), at] = hi
                u_hi[pl.ds(C, C), at] = lo
        build_onehot(oht_ref, cells_of(cell_ref, n))
        picked = dot_nn(u_hi[...], oht_ref[...])
        pg_ref[pl.ds(pl.multiple_of(n * C, C), C), :] = picked[:C] + picked[C:]
        return _

    each_sweep(sweep)


def pair_kernel(*refs, mode, stride, count):
    *ins, out_ref = refs
    keep_ref, got_ref = (ins[0].at[pl.ds(0, 8)], ins[0].at[pl.ds(8, 8)]) if len(ins) == 1 else ins
    peers = out_ref.shape[0] // stride
    mine, other = keep_ref[pl.ds(0, 1), :], got_ref[pl.ds(0, 1), :]
    both = mine + other
    lane = lax.broadcasted_iota(jnp.int32, (1, 128), 1)

    def swap(v):
        return pltpu.roll(jnp.broadcast_to(v, (8, 128)), C, 1)[:1]

    if mode == "stats":
        gap = mine - other
        both = jnp.where(lane < C, 0.5 * both, both + (0.5 * NPOS) * swap(gap * gap))
    if mode == "pillars":
        m_num, o_num = keep_ref[pl.ds(1, 1), :], got_ref[pl.ds(1, 1), :]
        number = m_num + o_num
        gap = mine / m_num - other / o_num
        both = jnp.where(lane < C, both, both + (m_num * o_num / number) * swap(gap * gap))
        out_ref[pl.ds(1, peers, stride=stride), :] = jnp.broadcast_to(number, (peers, 128))
    row = jnp.broadcast_to(both, (peers, 128))
    if stride == 1:
        out_ref[...] = row
    else:
        out_ref[pl.ds(0, peers, stride=stride), :] = row
    for j in range(count):
        at = pl.ds(8 + j * peers, peers)
        out_ref[pl.ds(1 + j, peers, stride=stride), :] = keep_ref[at, :] + got_ref[at, :]


def assemble_kernel(mine_ref, theirs_ref, out_ref, *, peers):
    first = first_core()
    count = BLOCK // peers
    per_peer = (LAYERS + 1) * count

    def halves(at):
        mine, theirs = mine_ref[at, :], theirs_ref[at, :]
        return jnp.where(first, mine, theirs), jnp.where(first, theirs, mine)

    for l in range(LAYERS):
        for j in range(count):
            for h, rows in enumerate(halves(pl.ds(l * count + j, peers, stride=per_peer))):
                out_ref[pl.ds((h * BLOCK + j * peers) * LAYERS + l, peers, stride=LAYERS), :] = rows
        size = min(peers, TAP_ROWS)
        for step in range(0, TAP_ROWS, size):
            start = max(l - 1, 0) * TAP_ROWS + step
            at = pl.ds(start % peers * per_peer + LAYERS * count + start // peers, size, stride=per_peer)
            rows = halves(at)[0 if l == 0 else 1]
            out_ref[pl.ds((2 * BLOCK + step) * LAYERS + l, size, stride=LAYERS), :] = rows


def call(kernel, name, outs, args, scratch=(), scalar=False, copies=False, **params):
    specs = [pl.BlockSpec(memory_space=pltpu.HBM if copies else pltpu.VMEM)] * len(args)
    if scalar:
        specs[0] = pl.BlockSpec(memory_space=pltpu.SMEM)
    return pl.pallas_call(
        functools.partial(kernel, **params) if params else kernel,
        name=name,
        out_shape=tuple(jax.ShapeDtypeStruct(shape, dtype) for shape, dtype in outs),
        in_specs=specs,
        scratch_shapes=[pltpu.VMEM(shape, dtype) for shape, dtype in scratch]
        + [pltpu.SemaphoreType.DMA((len(args),))] * copies,
        compiler_params=pltpu.CompilerParams(vmem_limit_bytes=20 << 20),
        interpret=INTERPRET,
    )(*args)


def partner(v):
    return lax.ppermute(v, "k", [(0, 1), (1, 0)])


def to_peers(rows, peers):
    sent = rows.reshape(peers, -1, 1, 128)
    return lax.all_to_all(sent, WIDE, 0, 0, tiled=True).reshape(-1, 128)


def exchange(name, mode, keep, send, peers, stride=1, count=0):
    pair = (keep, partner(send)) if send is not None else (lax.all_gather(keep, "k", tiled=True),)
    (out,) = call(
        pair_kernel, name, [((peers * stride, 128), F32)], pair, mode=mode, stride=stride, count=count
    )
    return to_peers(out, peers)


def per_device(
    points, counts, cells, pfn_weight, pfn_gain, pfn_bias, conv_weight, bn_gain, bn_bias, cotangent,
    *, sizes,
):
    peers = sizes["x"] * sizes["y"] * sizes["z"]
    count = BLOCK // peers
    w = conv_weight.reshape(LAYERS, 9, TAP_ROWS, 128).transpose(1, 2, 0, 3).reshape(9 * TAP_ROWS * LAYERS, 128)
    row = ((1, 128), F32)
    rows8 = ((8, 128), F32)
    tile = ((128, 128), F32)
    plane = ((C, NPOS), F32)
    pad = ((3 * C, NS * PADW), BF16)
    buf = ((C, C), F32)
    end = ((TAP_ROWS, 128), F32)

    hmax, part = call(
        pfn_kernel, "pfn", [((C, NS * PILL), F32), rows8],
        (points.reshape(NS * 4 * MAXP, PILL), counts, cells, pfn_weight),
        [((C, NS * PILL), F32), tile, ((NS * 4 * MAXP, PILL), F32), ((NS, PILL), jnp.int32), ((NS, PILL), jnp.int32), ((9, C), F32)],
        copies=True,
    )
    got = exchange("pair_p", "pillars", part, None, peers, 2)
    ev = ((3 * C, NS * POS), BF16)
    od = ((3 * C, NS * (POS + OW)), BF16)
    z, part, *grid0 = call(
        first_conv_kernel, "conv0", [plane, rows8, ev, ev, od, od],
        (got, hmax, cells, pfn_gain[None], pfn_bias[None], w),
        [((GH * GW, PILL), BF16), ((2 * C, GH * GW), F32), buf],
    )
    pre = [z]
    stats = []
    for l in range(1, LAYERS):
        got = exchange("pair_s", "stats", part, None, peers)
        z, part, st = call(
            conv_kernel, "conv", [plane, rows8, tile],
            (jnp.full((1,), l, jnp.int32), got, pre[-1], bn_gain, bn_bias, w), [pad, pad, buf], scalar=True,
        )
        pre.append(z)
        stats.append(st)
    got = exchange("pair_s", "stats", part, part, peers)
    slab = ((NS * C * OH, OW), F32)
    payload = ((8 + 4 * BLOCK, 128), F32)
    feat, gy, keep, send, st = call(
        turn_kernel, "turn", [slab, plane, payload, payload, tile],
        (got, pre[-1], bn_gain, bn_bias, cotangent.reshape(NS * C * OH, OW), pre[0], stats[0], *grid0),
        [buf],
    )
    stats.append(st)
    sums = [None] * LAYERS
    reds = [None] * LAYERS
    ends = []
    blocks = 4
    for l in range(LAYERS - 1, 0, -1):
        got = exchange(f"pair_g{blocks}", "sums", keep, send, peers, 1 + blocks * count, blocks * count)
        after = 4 if l == 1 else 1
        payload = ((8 + after * BLOCK, 128), F32)
        gy, keep, send, sums[l], reds[l], *end_rows = call(
            back_kernel, f"back{l}", [plane, payload, payload, row, ((blocks * count, 128), F32)] + [end] * (l > 1),
            (got, pre[l], gy, stats[l], bn_gain, bn_bias, pre[l - 1], stats[l - 1], w)
            + ((*grid0, *ends) if l == 1 else ()),
            [pad, pad, pad, pad, plane, buf], layers=(l,), stride=1 + blocks * count,
        )
        ends += end_rows
        blocks = after
    got = exchange(f"pair_g{blocks}", "sums", keep, send, peers, 1 + blocks * count, blocks * count)
    tbuf = ((2 * C, POS + OW), BF16)
    pillar_grad, norm_grads, own = call(
        last_back_kernel, "back0",
        [((NS * C, PILL), F32), ((2 * LAYERS, C), F32), (((LAYERS + 1) * count, 128), F32)],
        (got, pre[0], gy, stats[0], bn_gain, bn_bias, cells, w, reds[3], reds[2], reds[1], *sums[1:]),
        [tbuf, tbuf, ((2 * C, GH * GW), BF16), ((GH * GW, PILL), BF16), buf], stride=1 + blocks * count,
    )
    rows = (LAYERS + 1) * count
    mine = to_peers(jnp.broadcast_to(own[None], (peers, rows, 128)).reshape(peers * rows, 128), peers)
    (total,) = call(
        assemble_kernel, "assemble", [((9 * TAP_ROWS * LAYERS, 128), F32)], (mine, partner(mine)), peers=peers
    )
    total = total.reshape(9, TAP_ROWS, LAYERS, 128).transpose(2, 0, 1, 3).reshape(LAYERS, 9, C * C)
    return (
        feat.reshape(NS, C, OH, OW),
        total,
        norm_grads.reshape(2, LAYERS, C),
        pillar_grad.reshape(NS, C, PILL),
    )


def build(finer):
    sizes = dict(finer.shape)
    split4 = P(ALL, None, None, None)
    return jax.shard_map(
        functools.partial(per_device, sizes=sizes),
        mesh=finer,
        in_specs=(split4, P(ALL, None), P(ALL, None), P(), P(), P(), P(), P(), P(), split4),
        out_specs=(split4, P(), P(), P(ALL, None, None)),
        check_vma=False,
    )


def solution(mesh):
    return build(Mesh(mesh.devices.reshape(4, 2, 4, 8), ALL))
```

profile of v0, /device:TPU:1, one launch (start us, length us, event | category | flops | bytes accessed | tf_op | source)
XLA Modules:
  0.0 255.4 jit_solution(16228236552320607992)
XLA Ops:
  3.7 2.7 %pfn.1 = (f32[64,512]{1,0:T(8,128)S(1)}, f32[8,128]{1,0:T(8,128)S(1)}) custom-call(f32[256,256]{1,0:T(8,128)S(1)} %bitcast.73, s32[2,256]{1,0:T(2,128)S(1)} %copy-done.8, s32[2,256]{1,0:T(2,128)S(1)} %copy-done.5, f32[9,64]{1,0:T(8,128)S(1)} %copy-done.7), custom_call_target="tpu_custom_call" | custom-call | tf_op jit(solution)/shard_map/pfn/pallas_call | solution.py:687
  6.4 4.7 %all_gather.12.refs_0_ = f32[16,128]{1,0:T(8,128)S(1)} all-gather(f32[8,128]{1,0:T(8,128)S(1)} %get-tuple-element.46), channel_id=1, replica_groups=mesh['x'=4,'k'=2,'y'=4,'z'=8] {'k'}, dimensions={0}, use_global_device_ids=true | all-gather | bytes 12288 | tf_op jit(solution)/shard_map/all_gather | solution.py:709
  11.2 25.1 %all_to_all.50 = f32[128,2,1,128]{3,1,2,0:T(2,128)S(1)} all-to-all(f32[128,2,1,128]{3,1,2,0:T(2,128)S(1)} %bitcast.67), channel_id=1, replica_groups=mesh['x'=4,'k'=2,'y'=4,'z'=8] {'x','y','z'}, dimensions={0} | all-to-all | bytes 262144 | tf_op jit(solution)/shard_map/all_to_all | solution.py:705
  37.0 2.4 conv0.1
  39.4 3.2 %all_gather.13.refs_0_ = f32[16,128]{1,0:T(8,128)S(1)} all-gather(f32[8,128]{1,0:T(8,128)S(1)} %get-tuple-element.48), channel_id=1, replica_groups=mesh['x'=4,'k'=2,'y'=4,'z'=8] {'k'}, dimensions={0}, use_global_device_ids=true | all-gather | bytes 12288 | tf_op jit(solution)/shard_map/all_gather | solution.py:709
  42.7 16.2 %all_to_all.51 = f32[128,1,1,128]{3,2,1,0:T(1,128)S(1)} all-to-all(f32[128,1,1,128]{3,2,1,0:T(1,128)S(1)} %bitcast.75), channel_id=1, replica_groups=mesh['x'=4,'k'=2,'y'=4,'z'=8] {'x','y','z'}, dimensions={0} | all-to-all | bytes 131072 | tf_op jit(solution)/shard_map/all_to_all | solution.py:705
  59.6 2.1 conv.3
  61.7 3.1 %all_gather.14.refs_0_ = f32[16,128]{1,0:T(8,128)S(1)} all-gather(f32[8,128]{1,0:T(8,128)S(1)} %get-tuple-element.50), channel_id=1, replica_groups=mesh['x'=4,'k'=2,'y'=4,'z'=8] {'k'}, dimensions={0}, use_global_device_ids=true | all-gather | bytes 12288 | tf_op jit(solution)/shard_map/all_gather | solution.py:709
  64.8 16.1 %all_to_all.52 = f32[128,1,1,128]{3,2,1,0:T(1,128)S(1)} all-to-all(f32[128,1,1,128]{3,2,1,0:T(1,128)S(1)} %bitcast.76), channel_id=1, replica_groups=mesh['x'=4,'k'=2,'y'=4,'z'=8] {'x','y','z'}, dimensions={0} | all-to-all | bytes 131072 | tf_op jit(solution)/shard_map/all_to_all | solution.py:705
  80.9 2.1 conv.4
  83.1 3.0 %all_gather.15.refs_0_ = f32[16,128]{1,0:T(8,128)S(1)} all-gather(f32[8,128]{1,0:T(8,128)S(1)} %get-tuple-element.52), channel_id=1, replica_groups=mesh['x'=4,'k'=2,'y'=4,'z'=8] {'k'}, dimensions={0}, use_global_device_ids=true | all-gather | bytes 12288 | tf_op jit(solution)/shard_map/all_gather | solution.py:709
  86.2 16.1 %all_to_all.53 = f32[128,1,1,128]{3,2,1,0:T(1,128)S(1)} all-to-all(f32[128,1,1,128]{3,2,1,0:T(1,128)S(1)} %bitcast.77), channel_id=1, replica_groups=mesh['x'=4,'k'=2,'y'=4,'z'=8] {'x','y','z'}, dimensions={0} | all-to-all | bytes 131072 | tf_op jit(solution)/shard_map/all_to_all | solution.py:705
  107.1 16.1 %all_to_all.54 = f32[128,1,1,128]{3,2,1,0:T(1,128)S(1)} all-to-all(f32[128,1,1,128]{3,2,1,0:T(1,128)S(1)} %bitcast.74), channel_id=1, replica_groups=mesh['x'=4,'k'=2,'y'=4,'z'=8] {'x','y','z'}, dimensions={0} | all-to-all | bytes 131072 | tf_op jit(solution)/shard_map/all_to_all | solution.py:705
  123.2 3.1 %turn.1 = (f32[512,128]{1,0:T(8,128)}, f32[64,1024]{1,0:T(8,128)S(1)}, f32[520,128]{1,0:T(8,128)S(1)}, f32[520,128]{1,0:T(8,128)S(1)}, f32[128,128]{1,0:T(8,128)S(1)}) custom-call(f32[128,128]{1,0:T(8,128)S(1)} %bitcast.79, f32[64,1024]{1,0:T(8,128)S(1)} %get-tuple-element.55.z_ref, f32[4,64]{1,0:T(4,128)S(1)} %copy-done.3, f32[4,64]{1,0:T(4,128)S(1)} %copy-done.4, ...), custom_call_target="tpu_custom_call" | custom-call | tf_op jit(solution)/shard_map/turn/pallas_call | solution.py:687
  129.1 21.0 %all_to_all.55 = f32[128,5,1,128]{3,2,1,0:T(1,128)S(1)} all-to-all(f32[128,5,1,128]{3,2,1,0:T(1,128)S(1)} %bitcast.59), channel_id=1, replica_groups=mesh['x'=4,'k'=2,'y'=4,'z'=8] {'x','y','z'}, dimensions={0} | all-to-all | bytes 655360 | tf_op jit(solution)/shard_map/all_to_all | solution.py:705
  150.1 3.7 %back3.1 = (f32[64,1024]{1,0:T(8,128)S(1)}, f32[136,128]{1,0:T(8,128)S(1)}, f32[136,128]{1,0:T(8,128)S(1)}, f32[1,128]{1,0:T(1,128)S(1)}, f32[4,128]{1,0:T(4,128)S(1)}, /*index=5*/f32[32,128]{1,0:T(8,128)S(1)}) custom-call(f32[640,128]{1,0:T(8,128)S(1)} %bitcast.58, f32[64,1024]{1,0:T(8,128)S(1)} %get-tuple-element.55.z_ref, ...), custom_call_target="tpu_custom_call" | custom-call | tf_op jit(solution)/shard_map/back3/pallas_call | solution.py:687
  156.8 17.3 %all_to_all.56 = f32[128,2,1,128]{3,1,2,0:T(2,128)S(1)} all-to-all(f32[128,2,1,128]{3,1,2,0:T(2,128)S(1)} %bitcast.65), channel_id=1, replica_groups=mesh['x'=4,'k'=2,'y'=4,'z'=8] {'x','y','z'}, dimensions={0} | all-to-all | bytes 262144 | tf_op jit(solution)/shard_map/all_to_all | solution.py:705
  174.0 3.7 %back2.1 = (f32[64,1024]{1,0:T(8,128)S(1)}, f32[136,128]{1,0:T(8,128)S(1)}, f32[136,128]{1,0:T(8,128)S(1)}, f32[1,128]{1,0:T(1,128)S(1)}, f32[1,128]{1,0:T(1,128)S(1)}, /*index=5*/f32[32,128]{1,0:T(8,128)S(1)}) custom-call(f32[256,128]{1,0:T(8,128)S(1)} %bitcast.64, f32[64,1024]{1,0:T(8,128)S(1)} %get-tuple-element.53.z_ref.zp_ref, ...), custom_call_target="tpu_custom_call" | custom-call | tf_op jit(solution)/shard_map/back2/pallas_call | solution.py:687
  180.2 17.4 %all_to_all.57 = f32[128,2,1,128]{3,1,2,0:T(2,128)S(1)} all-to-all(f32[128,2,1,128]{3,1,2,0:T(2,128)S(1)} %bitcast.66), channel_id=1, replica_groups=mesh['x'=4,'k'=2,'y'=4,'z'=8] {'x','y','z'}, dimensions={0} | all-to-all | bytes 262144 | tf_op jit(solution)/shard_map/all_to_all | solution.py:705
  197.6 4.9 %back1.1 = (f32[64,1024]{1,0:T(8,128)S(1)}, f32[520,128]{1,0:T(8,128)S(1)}, f32[520,128]{1,0:T(8,128)S(1)}, f32[1,128]{1,0:T(1,128)S(1)}, f32[1,128]{1,0:T(1,128)S(1)}) custom-call(f32[256,128]{1,0:T(8,128)S(1)} %bitcast.69, f32[64,1024]{1,0:T(8,128)S(1)} %get-tuple-element.51.z_ref.zp_ref, f32[64,1024]{1,0:T(8,128)S(1)} %get-tuple-element.73.gy_ref, ...), custom_call_target="tpu_custom_call" | custom-call | tf_op jit(solution)/shard_map/back1/pallas_call | solution.py:687
  205.4 21.0 %all_to_all.58 = f32[128,5,1,128]{3,2,1,0:T(1,128)S(1)} all-to-all(f32[128,5,1,128]{3,2,1,0:T(1,128)S(1)} %bitcast.60), channel_id=1, replica_groups=mesh['x'=4,'k'=2,'y'=4,'z'=8] {'x','y','z'}, dimensions={0} | all-to-all | bytes 655360 | tf_op jit(solution)/shard_map/all_to_all | solution.py:705
  226.4 3.2 %back0.1 = (f32[128,256]{1,0:T(8,128)}, f32[8,64]{1,0:T(8,128)}, f32[5,128]{1,0:T(8,128)S(1)}) custom-call(f32[640,128]{1,0:T(8,128)S(1)} %bitcast.61, f32[64,1024]{1,0:T(8,128)S(1)} %get-tuple-element.49.z_ref.z0_ref.zp_ref, f32[64,1024]{1,0:T(8,128)S(1)} %get-tuple-element.78.gy_ref, f32[128,128]{1,0:T(8,128)S(1)} %get-tuple-element.56.stats0_ref.statsp_ref.stats_ref, ...), custom_call_target="tpu_custom_call" | custom-call | tf_op jit(solution)/shard_map/back0/pallas_call | solution.py:687
  229.8 20.5 %all_to_all.59 = f32[128,5,1,128]{3,2,1,0:T(1,128)S(1)} all-to-all(f32[128,5,1,128]{3,2,1,0:T(1,128)S(1)} %reshape_reshape.3), channel_id=1, replica_groups=mesh['x'=4,'k'=2,'y'=4,'z'=8] {'x','y','z'}, dimensions={0} | all-to-all | bytes 655360 | tf_op jit(solution)/shard_map/all_to_all | solution.py:705
  250.3 3.0 %collective-permute-start.5 = (f32[640,128]{1,0:T(8,128)S(1)}, f32[640,128]{1,0:T(8,128)S(1)}, u32[]{:S(2)}, u32[]{:S(2)}) collective-permute-start(f32[640,128]{1,0:T(8,128)S(1)} %bitcast.62), channel_id=1, source_target_pairs={{0,32},{32,0},{1,33},{33,1},{2,34},{34,2},{3,35},{35,3},{4,36},{36... | collective-permute-start | bytes 983048 | tf_op jit(solution)/shard_map/ppermute | solution.py:700
  (45 shorter events, 23.0 us)
Async XLA Ops:
  0.6 35.7 %copy-start = (f32[4,9,4096]{2,0,1:T(4,128)S(1)}, f32[4,9,4096]{2,0,1:T(4,128)}, u32[]{:S(2)}) copy-start(f32[4,9,4096]{2,0,1:T(4,128)} %param.16) | copy-start | bytes 1769476
  0.6 1.0 copy-start.1
  1.7 0.7 copy-start.5
  2.3 0.7 copy-start.7
  3.0 0.7 copy-start.8
  36.3 0.7 copy-start.6
  36.3 0.7 copy-start.9
  36.3 0.7 copy-start.10
  42.7 16.2 %copy-start.4 = (f32[4,64]{1,0:T(4,128)S(1)}, f32[4,64]{1,0:T(4,128)}, u32[]{:S(2)}) copy-start(f32[4,64]{1,0:T(4,128)} %bias_ref.15) | copy-start | bytes 3076
  58.9 0.7 copy-start.3
  102.3 21.0 %copy-start.2 = (f32[2,64,4,128]{3,2,1,0:T(4,128)S(1)}, f32[2,64,4,128]{3,2,1,0:T(4,128)}, u32[]{:S(2)}) copy-start(f32[2,64,4,128]{3,2,1,0:T(4,128)} %param.19) | copy-start | bytes 786436
  104.4 2.7 %collective-permute-start = (f32[8,128]{1,0:T(8,128)S(1)}, f32[8,128]{1,0:T(8,128)S(1)}, u32[]{:S(2)}, u32[]{:S(2)}) collective-permute-start(f32[8,128]{1,0:T(8,128)S(1)} %get-tuple-element.54.refs_0_), channel_id=1, source_target_pairs={{0,32},{32,0},{1,33},{33,1},{2,34},{34,2},{3,35},{35,3},{4,36},{36... | collective-permute-start | bytes 12296 | tf_op jit(solution)/shard_map/ppermute | solution.py:700
  126.3 2.7 %collective-permute-start.1 = (f32[520,128]{1,0:T(8,128)S(1)}, f32[520,128]{1,0:T(8,128)S(1)}, u32[]{:S(2)}, u32[]{:S(2)}) collective-permute-start(f32[520,128]{1,0:T(8,128)S(1)} %get-tuple-element.63), channel_id=1, source_target_pairs={{0,32},{32,0},{1,33},{33,1},{2,34},{34,2},{3,35},{35,3},{4,36},{36... | collective-permute-start | bytes 798728 | tf_op jit(solution)/shard_map/ppermute | solution.py:700
  153.8 2.9 %collective-permute-start.2 = (f32[136,128]{1,0:T(8,128)S(1)}, f32[136,128]{1,0:T(8,128)S(1)}, u32[]{:S(2)}, u32[]{:S(2)}) collective-permute-start(f32[136,128]{1,0:T(8,128)S(1)} %get-tuple-element.68), channel_id=1, source_target_pairs={{0,32},{32,0},{1,33},{33,1},{2,34},{34,2},{3,35},{35,3},{4,36},{36... | collective-permute-start | bytes 208904 | tf_op jit(solution)/shard_map/ppermute | solution.py:700
  177.7 2.5 collective-permute-start.3
  202.6 2.8 %collective-permute-start.4 = (f32[520,128]{1,0:T(8,128)S(1)}, f32[520,128]{1,0:T(8,128)S(1)}, u32[]{:S(2)}, u32[]{:S(2)}) collective-permute-start(f32[520,128]{1,0:T(8,128)S(1)} %get-tuple-element.77), channel_id=1, source_target_pairs={{0,32},{32,0},{1,33},{33,1},{2,34},{34,2},{3,35},{35,3},{4,36},{36... | collective-permute-start | bytes 798728 | tf_op jit(solution)/shard_map/ppermute | solution.py:700
  250.3 4.3 %collective-permute-start.5 = (f32[640,128]{1,0:T(8,128)S(1)}, f32[640,128]{1,0:T(8,128)S(1)}, u32[]{:S(2)}, u32[]{:S(2)}) collective-permute-start(f32[640,128]{1,0:T(8,128)S(1)} %bitcast.62), channel_id=1, source_target_pairs={{0,32},{32,0},{1,33},{33,1},{2,34},{34,2},{3,35},{35,3},{4,36},{36... | collective-permute-start | bytes 983048 | tf_op jit(solution)/shard_map/ppermute | solution.py:700
where the time goes:
time: 256 us; the launch traced here: 255 us
  blocking collectives  201 us (79%)
  Pallas kernels  31.5 us (12%)
  starting transfers between devices  11.6 us (5%)
  waiting for transfers between devices  6.23 us (2%)
  local copies, waits for them, and re-layouts  4.6 us (2%)
    all_to_all x10, blocking collectives, to_peers(): return lax.all_to_all(sent, WIDE, 0, 0, tiled=True).reshape(-1, 128)  187 us
    pallas_call x20, Pallas kernels, call(): pl.pallas_call(functools.partial(kernel, **params) if params else kernel,...  31.5 us
    all_gather x4, blocking collectives, exchange(): lax.all_gather(keep, 'k', tiled=True)  13.9 us
    ppermute x6, starting transfers between devices, partner(): return lax.ppermute(v, 'k', [(0, 1), (1, 0)])  11.6 us
    ppermute x6, waiting for transfers between devices, partner(): return lax.ppermute(v, 'k', [(0, 1), (1, 0)])  6.23 us
  transfers between devices with their start and end apart: 6, of which 6 were waited for; matrix products, arithmetic and copies ran while one was open for 0% of the time, Pallas kernels for 0%

commit v1 on v0

--- a/solution.py
+++ b/solution.py
@@ -28,6 +28,9 @@
 ALL = ("x", "k", "y", "z")
 WIDE = ("x", "y", "z")
 INTERPRET = False
+GB_ROW = C
+TARGET_ROW = C + 8
+KEPT_ROWS = C + 16
 
 
 def split(v):
@@ -70,6 +73,8 @@
 
 
 def lanes_from(start, size=OW):
+    if isinstance(start, int):
+        return pl.ds(start, size)
     return pl.ds(pl.multiple_of(start, 128), size)
 
 
@@ -78,19 +83,14 @@
 
 
 def each_row(body):
-    def step(t, _):
-        n = lax.div(t, OH)
-        body(lanes_from(t * OW), n, t - n * OH)
-        return _
-
-    lax.fori_loop(0, NS * OH, step, 0)
+    for t in range(NS * OH):
+        body(lanes_from(t * OW), t // OH, t % OH)
 
 
 def put(hi_ref, lo_ref, row, col, v):
     hi, lo = split(v)
-    col = pl.multiple_of(col, 128)
-    hi_ref[pl.ds(row, C), pl.ds(col, 128)] = hi
-    lo_ref[pl.ds(row, C), pl.ds(col, 128)] = lo
+    hi_ref[pl.ds(row, C), lanes_from(col)] = hi
+    lo_ref[pl.ds(row, C), lanes_from(col)] = lo
 
 
 def put_shifted(hi_ref, lo_ref, n, r, v, lane):
@@ -113,33 +113,24 @@
     return p[:C, :POS] + p[C : 2 * C, OW : OW + POS] + p[2 * C :, 2 * OW : 2 * OW + POS]
 
 
-def choose(layer, layers, read):
-    value = read(layers[0])
-    for l in layers[1:]:
-        value = jnp.where(layer == l, read(l), value)
-    return value
-
-
-def tap_block(w_ref, buf_ref, layer, layers, tap):
-    packed = choose(
-        layer, layers, lambda l: w_ref[pl.ds(tap * TAP_ROWS * LAYERS + l, TAP_ROWS, stride=LAYERS), :]
-    )
+def tap_block(w_ref, buf_ref, layer, tap):
+    packed = w_ref[pl.ds(tap * TAP_ROWS * LAYERS + layer, TAP_ROWS, stride=LAYERS), :]
     buf_ref[pl.ds(0, TAP_ROWS, stride=2), :] = packed[:, :C]
     buf_ref[pl.ds(1, TAP_ROWS, stride=2), :] = packed[:, C:]
     return buf_ref[...]
 
 
-def forward_weights(w_ref, buf_ref, layer, layers):
+def forward_weights(w_ref, buf_ref, layer):
     rows = []
     for a in range(3):
-        rows.append(jnp.concatenate([tap_block(w_ref, buf_ref, layer, layers, 3 * a + b) for b in range(3)], axis=1))
+        rows.append(jnp.concatenate([tap_block(w_ref, buf_ref, layer, 3 * a + b) for b in range(3)], axis=1))
     return jnp.concatenate(rows, axis=0)
 
 
-def backward_weights(w_ref, buf_ref, layer, layers):
+def backward_weights(w_ref, buf_ref, layer):
     rows = []
     for a in range(3):
-        blocks = [jnp.transpose(tap_block(w_ref, buf_ref, layer, layers, 3 * (2 - a) + 2 - b)) for b in range(3)]
+        blocks = [jnp.transpose(tap_block(w_ref, buf_ref, layer, 3 * (2 - a) + 2 - b)) for b in range(3)]
         rows.append(jnp.concatenate(blocks, axis=1))
     return jnp.concatenate(rows, axis=0)
 
@@ -147,18 +138,14 @@
 def first_backward_weights(w_ref, buf_ref):
     rows = []
     for a in range(3):
-        left, mid, right = (jnp.transpose(tap_block(w_ref, buf_ref, 0, (0,), 3 * a + b)) for b in range(3))
+        left, mid, right = (jnp.transpose(tap_block(w_ref, buf_ref, 0, 3 * a + b)) for b in range(3))
         rows.append(jnp.concatenate([mid, jnp.zeros((C, C), F32)], axis=1))
         rows.append(jnp.concatenate([right, left], axis=1))
     return jnp.concatenate(rows, axis=0)
 
 
-def gain_bias(gain_ref, bias_ref, layer, layers):
-    def row(l):
-        at = pl.ds(l, 1)
-        return jnp.concatenate([gain_ref[at, :], bias_ref[at, :]], axis=1)
-
-    gb = columns(choose(layer, layers, row))
+def gain_bias(gb_ref, row):
+    gb = columns(gb_ref[pl.ds(GB_ROW + row, 1), pl.ds(0, 128)])
     return gb[:C], gb[C:]
 
 
@@ -225,17 +212,29 @@
     return jnp.where(lane < C, mean, lax.rsqrt(var + EPS))
 
 
-def pfn_kernel(pts_in, cnt_in, cell_in, w_in, hmax_ref, part_ref, base_ref, w_pad, pts_ref, cnt_ref, cell_ref, w_ref, sems):
+def pfn_kernel(
+    pts_in, cnt_in, cell_in, w_in, gain_in, bias_in, pgain_in, pbias_in,
+    kept_ref, part_ref,
+    base_ref, w_pad, pts_ref, cnt_ref, cell_ref, w_ref, gain_ref, bias_ref, pgain_ref, pbias_ref, sems,
+):
     copies = [
         pltpu.make_async_copy(src, dst, sems.at[i])
         for i, (src, dst) in enumerate(
-            ((pts_in, pts_ref), (cnt_in, cnt_ref), (cell_in, cell_ref), (w_in, w_ref))
+            (
+                (pts_in, pts_ref), (cnt_in, cnt_ref), (cell_in, cell_ref), (w_in, w_ref),
+                (gain_in, gain_ref), (bias_in, bias_ref), (pgain_in, pgain_ref), (pbias_in, pbias_ref),
+            )
         )
     ]
     for copy in copies:
         copy.start()
     for copy in copies:
         copy.wait()
+    kept_ref[pl.ds(GB_ROW, 16), :] = jnp.zeros((16, NS * PILL), F32)
+    lanes = pl.ds(0, 128)
+    kept_ref[pl.ds(GB_ROW, LAYERS), lanes] = jnp.concatenate([gain_ref[...], bias_ref[...]], axis=1)
+    kept_ref[pl.ds(GB_ROW + LAYERS, 1), lanes] = jnp.concatenate([pgain_ref[...], pbias_ref[...]], axis=1)
+    kept_ref[pl.ds(TARGET_ROW, NS), pl.ds(0, PILL)] = target_lane(cell_ref[...]).astype(F32)
     w_pad[...] = jnp.zeros((128, 128), F32)
     w_pad[pl.ds(0, 9), pl.ds(0, C)] = w_ref[...]
     w_cols = jnp.transpose(w_pad[...])
@@ -282,30 +281,31 @@
         bz = jnp.broadcast_to(wz[ch], (half, 128))
         br = jnp.broadcast_to(wr[ch], (half, 128))
         mb = jnp.broadcast_to(mean[ch], (half, 128))
-        sq = jnp.zeros((half, 128), F32)
-        for n in range(NS):
-            for q in range(PILL // 128):
-                lanes = pl.ds(q * 128, 128)
-                base = base_ref[pl.ds(c0, half), pl.ds(n * PILL + q * 128, 128)] - mb
-                count = cnt_ref[pl.ds(n, 1), lanes]
-
-                def step(k8, carry, n=n, lanes=lanes, base=base, count=count, bx=bx, by=by, bz=bz, br=br):
-                    best, sq = carry
-                    p = [
-                        pts_ref[pl.ds(pl.multiple_of((n * 4 + j) * MAXP + k8 * 8, 8), 8), lanes]
-                        for j in range(4)
-                    ]
-                    for i in range(8):
-                        px, py, pz, pr = (v[i : i + 1] for v in p)
-                        d = bx * px + by * py + (bz * pz + br * pr) + base
-                        ok = jnp.broadcast_to(k8 * 8 + i < count, (half, 128))
-                        best = jnp.where(ok, jnp.maximum(best, d), best)
-                        sq = sq + jnp.where(ok, d * d, 0.0)
-                    return best, sq
-
-                start = jnp.full((half, 128), -3.0e38, F32)
-                best, sq = lax.fori_loop(0, MAXP // 8, step, (start, sq))
-                hmax_ref[pl.ds(c0, half), pl.ds(n * PILL + q * 128, 128)] = best + mb
+
+        def tile(t, sq, c0=c0, bx=bx, by=by, bz=bz, br=br, mb=mb):
+            n = lax.div(t, PILL // 128)
+            lanes = lanes_from((t - n * (PILL // 128)) * 128)
+            base = base_ref[pl.ds(c0, half), lanes_from(t * 128)] - mb
+            count = jnp.where(n == 0, cnt_ref[pl.ds(0, 1), lanes], cnt_ref[pl.ds(1, 1), lanes])
+
+            def step(k8, carry):
+                best, sq = carry
+                p = [
+                    pts_ref[pl.ds(pl.multiple_of((n * 4 + j) * MAXP + k8 * 8, 8), 8), lanes] for j in range(4)
+                ]
+                for i in range(8):
+                    px, py, pz, pr = (v[i : i + 1] for v in p)
+                    d = bx * px + by * py + (bz * pz + br * pr) + base
+                    ok = jnp.broadcast_to(k8 * 8 + i < count, (half, 128))
+                    best = jnp.where(ok, jnp.maximum(best, d), best)
+                    sq = sq + jnp.where(ok, d * d, 0.0)
+                return best, sq
+
+            best, sq = lax.fori_loop(0, MAXP // 8, step, (jnp.full((half, 128), -3.0e38, F32), sq))
+            kept_ref[pl.ds(c0, half), lanes_from(t * 128)] = best + mb
+            return sq
+
+        sq = lax.fori_loop(0, NS * PILL // 128, tile, jnp.zeros((half, 128), F32))
         sq_parts.append(sq)
     lane = lanes128()
     part_ref[pl.ds(0, 1), :] = to_row(
@@ -314,8 +314,10 @@
     part_ref[pl.ds(1, 1), :] = jnp.broadcast_to(number, (1, 128))
 
 
-def cells_of(cell_ref, n):
-    return jnp.where(n == 0, cell_ref[pl.ds(0, 1), :], cell_ref[pl.ds(1, 1), :])
+def targets_of(kept_ref, n):
+    at = pl.ds(0, PILL)
+    first, second = kept_ref[pl.ds(TARGET_ROW, 1), at], kept_ref[pl.ds(TARGET_ROW + 1, 1), at]
+    return jnp.where(n == 0, first, second).astype(jnp.int32)
 
 
 def target_lane(cell):
@@ -325,15 +327,20 @@
     return phase * POS + jnp.right_shift(row, 1) * OW + jnp.right_shift(col, 1)
 
 
-def build_onehot(oht_ref, cell):
-    target = jnp.broadcast_to(target_lane(cell), (256, PILL))
+def build_onehot(oht_ref, target):
+    wide = jnp.broadcast_to(target, (256, PILL))
     iota = lax.broadcasted_iota(jnp.int32, (256, PILL), 0)
-    for t in range(GH * GW // 256):
-        oht_ref[pl.ds(t * 256, 256), :] = jnp.where(iota + t * 256 == target, 1.0, 0.0).astype(BF16)
+
+    def step(t, _):
+        rows = pl.ds(pl.multiple_of(t * 256, 256), 256)
+        oht_ref[rows, :] = jnp.where(iota + t * 256 == wide, 1.0, 0.0).astype(BF16)
+        return _
+
+    lax.fori_loop(0, GH * GW // 256, step, 0)
 
 
 def first_conv_kernel(
-    g_ref, hmax_ref, cell_ref, gain_ref, bias_ref, w_ref,
+    g_ref, kept_ref, w_ref,
     z_ref, part_ref, ev_hi, ev_lo, od_hi, od_lo,
     oht_ref, place_ref, buf_ref,
 ):
@@ -348,17 +355,17 @@
     lane_row = lax.broadcasted_iota(jnp.int32, (1, 128), 1)
     stats = columns(jnp.where(lane_row < C, mean, lax.rsqrt(var + EPS)))
     mean_c, inv_c = stats[:C], stats[C:]
-    gain, bias = gain_bias(gain_ref, bias_ref, 0, (0,))
+    gain, bias = gain_bias(kept_ref, LAYERS)
     lane = lanes128()
-    w_hi, w_lo = split(forward_weights(w_ref, buf_ref, 0, (0,)))
+    w_hi, w_lo = split(forward_weights(w_ref, buf_ref, 0))
     outer_hi = jnp.concatenate([w_hi[:C], w_hi[2 * C :]], axis=0)
     outer_lo = jnp.concatenate([w_lo[:C], w_lo[2 * C :]], axis=0)
 
     def sweep(n, _):
-        build_onehot(oht_ref, cells_of(cell_ref, n))
+        build_onehot(oht_ref, targets_of(kept_ref, n))
         tiles = []
         for q in range(PILL // 128):
-            h = hmax_ref[:, lanes_from(n * PILL + q * 128)]
+            h = kept_ref[pl.ds(0, C), lanes_from(n * PILL + q * 128)]
             tiles.append(jnp.maximum(gain * (h - mean_c) * inv_c + bias, 0.0))
         p_hi, p_lo = split(jnp.concatenate(tiles, axis=1))
         place_ref[...] = dot_nt(jnp.concatenate([p_hi, p_lo], axis=0), oht_ref[...])
@@ -425,16 +432,15 @@
 
 
 def conv_kernel(
-    l_ref, g_ref, z_ref, gain_ref, bias_ref, w_ref, out_ref, part_ref, stats_ref, s_hi, s_lo, buf_ref
+    g_ref, z_ref, gb_ref, w_ref, out_ref, part_ref, stats_ref, s_hi, s_lo, buf_ref, *, layer
 ):
-    layer = l_ref[0]
     stats = columns(gathered_stats(g_ref[...]))
     stats_ref[...] = stats
     mean, inv = stats[:C], stats[C:]
-    gain, bias = gain_bias(gain_ref, bias_ref, layer - 1, (0, 1, 2))
+    gain, bias = gain_bias(gb_ref, layer - 1)
     lane = lanes128()
     zero_borders((s_hi, s_lo))
-    w_hi, w_lo = split(forward_weights(w_ref, buf_ref, layer, (1, 2, 3)))
+    w_hi, w_lo = split(forward_weights(w_ref, buf_ref, layer))
 
     def activate(at, n, r):
         y = gain * ((z_ref[:, at] - mean) * inv) + bias
@@ -450,14 +456,14 @@
 
 
 def turn_kernel(
-    g_ref, z_ref, gain_ref, bias_ref, ct_ref, z0_ref, stats0_ref, ev_hi, ev_lo, od_hi, od_lo,
+    g_ref, z_ref, gb_ref, ct_ref, z0_ref, stats0_ref, ev_hi, ev_lo, od_hi, od_lo,
     feat_ref, gy_ref, keep_ref, send_ref, stats_ref,
     buf_ref,
 ):
     stats = columns(gathered_stats(g_ref[...]))
     stats_ref[...] = stats
     mean, inv = stats[:C], stats[C:]
-    gain, bias = gain_bias(gain_ref, bias_ref, LAYERS - 1, (LAYERS - 1,))
+    gain, bias = gain_bias(gb_ref, LAYERS - 1)
     dy = jnp.zeros((C, 128), F32)
     dx = jnp.zeros((C, 128), F32)
     for n in range(NS):
@@ -495,27 +501,35 @@
     return gain * stats[C:], t[:C], t[C:], total
 
 
+def padded_grad_rows(s_hi, s_lo, a_hi, a_lo):
+    span = NS * PADW - 2 * OW
+    g_at = pl.ds(OW, span)
+    g_hi, g_lo = s_hi[pl.ds(C, C), g_at], s_lo[pl.ds(C, C), g_at]
+    return [
+        dot3(dot_nt, g_hi, g_lo, a_hi[:, pl.ds(a * OW, span)], a_lo[:, pl.ds(a * OW, span)]) for a in range(3)
+    ]
+
+
 def back_kernel(
-    g_ref, z_ref, gy_ref, stats_ref, gain_ref, bias_ref, zp_ref, statsp_ref, w_ref, *refs, layers, stride
+    g_ref, z_ref, gy_ref, stats_ref, gb_ref, zp_ref, statsp_ref, w_ref, *refs, layer, stride
 ):
-    (layer,) = layers
     if layer == 1:
         grid0, last3_ref, last2_ref, refs = refs[:4], refs[4], refs[5], refs[6:]
-    gyp_ref, keep_ref, send_ref, sums_ref, red_ref, *refs = refs
+    gyp_ref, sums_ref, red_ref, keep_ref, send_ref, *refs = refs
     if layer != 1:
         last_ref, *refs = refs
     s_hi, s_lo, a_hi, a_lo, slope_ref, buf_ref = refs
     reduced_rows(g_ref, stride, red_ref, red_ref.shape[0])
     stats = stats_ref[...]
     mean, inv = stats[:C], stats[C:]
-    gain, _ = gain_bias(gain_ref, bias_ref, layer, layers)
+    gain, _ = gain_bias(gb_ref, layer)
     scale, mean_dy, mean_dx, sums_ref[...] = grad_scales(rows_of(g_ref, stride, 0), stats, gain)
     statsp = statsp_ref[...]
     meanp, invp = statsp[:C], statsp[C:]
-    gainp, biasp = gain_bias(gain_ref, bias_ref, layer - 1, tuple(l - 1 for l in layers))
+    gainp, biasp = gain_bias(gb_ref, layer - 1)
     lane = lanes128()
     zero_borders((s_hi, s_lo, a_hi, a_lo))
-    w_hi, w_lo = split(backward_weights(w_ref, buf_ref, layer, layers))
+    w_hi, w_lo = split(backward_weights(w_ref, buf_ref, layer))
 
     def turn_back(at, n, r):
         xhat = (z_ref[:, at] - mean) * inv
@@ -543,22 +557,15 @@
     part = to_row(dy, dx)
     keep_ref[pl.ds(0, 1), :] = part
     send_ref[pl.ds(0, 1), :] = part
-    span = NS * PADW - 2 * OW
-    g_at = pl.ds(OW, span)
-    g_hi, g_lo = s_hi[pl.ds(C, C), g_at], s_lo[pl.ds(C, C), g_at]
-    rows = [
-        dot3(dot_nt, g_hi, g_lo, a_hi[:, pl.ds(a * OW, span)], a_lo[:, pl.ds(a * OW, span)]) for a in range(3)
-    ]
     refs = (keep_ref, send_ref)
-    last = store_kernel_grad(refs, 0, rows, buf_ref)
-    if layer == 1:
-        rows = first_grad_rows(lambda n: split(gyp_ref[:, lanes_from(n * POS, POS)]), grid0)
-        last0 = store_kernel_grad(refs, 1, rows, buf_ref)
-        none = jnp.zeros((TAP_ROWS, 128), F32)
-        store_half(refs, 2, [last0, none, none, none], [last, last2_ref[...], last3_ref[...], none])
-        store_half(refs, 3, [none] * 4, [none] * 4)
-    else:
+    last = store_kernel_grad(refs, 0, padded_grad_rows(s_hi, s_lo, a_hi, a_lo), buf_ref)
+    if layer != 1:
         last_ref[...] = last
+        return
+    rows = first_grad_rows(lambda n: split(gyp_ref[:, lanes_from(n * POS, POS)]), grid0)
+    last0 = store_kernel_grad(refs, 1, rows, buf_ref)
+    none = jnp.zeros((TAP_ROWS, 128), F32)
+    store_half(refs, 2, [last0, none, none, none], [last, last2_ref[...], last3_ref[...], none])
 
 
 def pick_channels(tile, pair, lane):
@@ -567,19 +574,17 @@
     return jnp.sum(jnp.where(row == want, tile, 0.0), axis=0, keepdims=True)
 
 
-def last_back_kernel(
-    g_ref, z_ref, gy_ref, stats_ref, gain_ref, bias_ref, cell_ref, w_ref,
-    first_red, red3, red2, sums1, sums2, sums3,
-    pg_ref, norm_ref, own_ref,
-    t_hi, t_lo, u_hi, oht_ref, buf_ref, *, stride,
+def own_rows_kernel(
+    g_ref, stats_ref, gb_ref, first_red, red3, red2, sums1, sums2, sums3, norm_ref, out_ref, scale_ref, *, stride
 ):
     stats = stats_ref[...]
-    mean, inv = stats[:C], stats[C:]
-    gain, _ = gain_bias(gain_ref, bias_ref, 0, (0,))
+    gain, _ = gain_bias(gb_ref, 0)
     scale, mean_dy, mean_dx, sums0 = grad_scales(rows_of(g_ref, stride, 0), stats, gain)
     for l, row in enumerate((sums0, sums1[...], sums2[...], sums3[...])):
         norm_ref[pl.ds(l, 1), :] = row[:, C:]
         norm_ref[pl.ds(LAYERS + l, 1), :] = row[:, :C]
+    for i, tile in enumerate((scale, mean_dy, mean_dx)):
+        scale_ref[pl.ds(i * C, C), :] = tile
     lane = lanes128()
     count = red3.shape[0]
     peers = BLOCK // count
@@ -599,7 +604,16 @@
         ends = jnp.where(first_core(), first_grad(ends, normed_end, plain_end, pair), ends)
         own = (first_grad(raw, normed, plain, pair), here, red2[pl.ds(j, 1), :], red3[pl.ds(j, 1), :], ends)
         for q in range(5):
-            own_ref[pl.ds(q * count + j, 1), :] = own[q]
+            at = pl.ds(q * count + j, peers, stride=5 * count)
+            out_ref[at, :] = jnp.broadcast_to(own[q], (peers, 128))
+
+
+def last_back_kernel(
+    z_ref, gy_ref, stats_ref, scale_ref, kept_ref, w_ref, pg_ref, t_hi, t_lo, u_hi, oht_ref, buf_ref
+):
+    mean, inv = stats_ref[pl.ds(0, C), :], stats_ref[pl.ds(C, C), :]
+    scale, mean_dy, mean_dx = (scale_ref[pl.ds(i * C, C), :] for i in range(3))
+    lane = lanes128()
     v_hi, v_lo = split(first_backward_weights(w_ref, buf_ref))
 
     def sweep(n, _):
@@ -621,7 +635,7 @@
                 hi, lo = split(u)
                 u_hi[pl.ds(0, C), at] = hi
                 u_hi[pl.ds(C, C), at] = lo
-        build_onehot(oht_ref, cells_of(cell_ref, n))
+        build_onehot(oht_ref, targets_of(kept_ref, n))
         picked = dot_nn(u_hi[...], oht_ref[...])
         pg_ref[pl.ds(pl.multiple_of(n * C, C), C), :] = picked[:C] + picked[C:]
         return _
@@ -629,10 +643,13 @@
     each_sweep(sweep)
 
 
-def pair_kernel(*refs, mode, stride, count):
+def pair_kernel(*refs, mode, stride):
     *ins, out_ref = refs
-    keep_ref, got_ref = (ins[0].at[pl.ds(0, 8)], ins[0].at[pl.ds(8, 8)]) if len(ins) == 1 else ins
     peers = out_ref.shape[0] // stride
+    if len(ins) == 1:
+        keep_ref, got_ref = ins[0].at[pl.ds(0, 8)], ins[0].at[pl.ds(8, 8)]
+    else:
+        keep_ref, got_ref = ins
     mine, other = keep_ref[pl.ds(0, 1), :], got_ref[pl.ds(0, 1), :]
     both = mine + other
     lane = lax.broadcasted_iota(jnp.int32, (1, 128), 1)
@@ -654,36 +671,32 @@
         out_ref[...] = row
     else:
         out_ref[pl.ds(0, peers, stride=stride), :] = row
-    for j in range(count):
-        at = pl.ds(8 + j * peers, peers)
+    for j, start in enumerate(range(8, keep_ref.shape[0], peers)):
+        at = pl.ds(start, peers)
         out_ref[pl.ds(1 + j, peers, stride=stride), :] = keep_ref[at, :] + got_ref[at, :]
 
 
-def assemble_kernel(mine_ref, theirs_ref, out_ref, *, peers):
-    first = first_core()
+def assemble_kernel(both_ref, out_ref, *, peers):
     count = BLOCK // peers
     per_peer = (LAYERS + 1) * count
 
-    def halves(at):
-        mine, theirs = mine_ref[at, :], theirs_ref[at, :]
-        return jnp.where(first, mine, theirs), jnp.where(first, theirs, mine)
+    def rows_at(core, start, size):
+        return both_ref[pl.ds(core * peers * per_peer + start, size, stride=per_peer), :]
 
     for l in range(LAYERS):
         for j in range(count):
-            for h, rows in enumerate(halves(pl.ds(l * count + j, peers, stride=per_peer))):
-                out_ref[pl.ds((h * BLOCK + j * peers) * LAYERS + l, peers, stride=LAYERS), :] = rows
+            for core in range(2):
+                at = pl.ds((core * BLOCK + j * peers) * LAYERS + l, peers, stride=LAYERS)
+                out_ref[at, :] = rows_at(core, l * count + j, peers)
         size = min(peers, TAP_ROWS)
         for step in range(0, TAP_ROWS, size):
             start = max(l - 1, 0) * TAP_ROWS + step
-            at = pl.ds(start % peers * per_peer + LAYERS * count + start // peers, size, stride=per_peer)
-            rows = halves(at)[0 if l == 0 else 1]
+            rows = rows_at(min(l, 1), start % peers * per_peer + LAYERS * count + start // peers, size)
             out_ref[pl.ds((2 * BLOCK + step) * LAYERS + l, size, stride=LAYERS), :] = rows
 
 
-def call(kernel, name, outs, args, scratch=(), scalar=False, copies=False, **params):
+def call(kernel, name, outs, args, scratch=(), copies=False, **params):
     specs = [pl.BlockSpec(memory_space=pltpu.HBM if copies else pltpu.VMEM)] * len(args)
-    if scalar:
-        specs[0] = pl.BlockSpec(memory_space=pltpu.SMEM)
     return pl.pallas_call(
         functools.partial(kernel, **params) if params else kernel,
         name=name,
@@ -691,7 +704,7 @@
         in_specs=specs,
         scratch_shapes=[pltpu.VMEM(shape, dtype) for shape, dtype in scratch]
         + [pltpu.SemaphoreType.DMA((len(args),))] * copies,
-        compiler_params=pltpu.CompilerParams(vmem_limit_bytes=20 << 20),
+        compiler_params=None if copies else pltpu.CompilerParams(vmem_limit_bytes=20 << 20),
         interpret=INTERPRET,
     )(*args)
 
@@ -705,11 +718,10 @@
     return lax.all_to_all(sent, WIDE, 0, 0, tiled=True).reshape(-1, 128)
 
 
-def exchange(name, mode, keep, send, peers, stride=1, count=0):
-    pair = (keep, partner(send)) if send is not None else (lax.all_gather(keep, "k", tiled=True),)
-    (out,) = call(
-        pair_kernel, name, [((peers * stride, 128), F32)], pair, mode=mode, stride=stride, count=count
-    )
+def exchange(name, mode, keep, peers, send=None):
+    pair = (lax.all_gather(keep, "k", tiled=True),) if send is None else (keep, partner(send))
+    rows = (2 if mode == "pillars" else 1) + (keep.shape[0] - 8) // peers
+    (out,) = call(pair_kernel, name, [((peers * rows, 128), F32)], pair, mode=mode, stride=rows)
     return to_peers(out, peers)
 
 
@@ -728,67 +740,72 @@
     buf = ((C, C), F32)
     end = ((TAP_ROWS, 128), F32)
 
-    hmax, part = call(
-        pfn_kernel, "pfn", [((C, NS * PILL), F32), rows8],
-        (points.reshape(NS * 4 * MAXP, PILL), counts, cells, pfn_weight),
-        [((C, NS * PILL), F32), tile, ((NS * 4 * MAXP, PILL), F32), ((NS, PILL), jnp.int32), ((NS, PILL), jnp.int32), ((9, C), F32)],
+    ints = ((NS, PILL), jnp.int32)
+    vectors = [((LAYERS, C), F32)] * 2 + [((1, C), F32)] * 2
+    kept, part = call(
+        pfn_kernel, "pfn", [((KEPT_ROWS, NS * PILL), F32), rows8],
+        (
+            points.reshape(NS * 4 * MAXP, PILL), counts, cells, pfn_weight,
+            bn_gain, bn_bias, pfn_gain[None], pfn_bias[None],
+        ),
+        [((C, NS * PILL), F32), tile, ((NS * 4 * MAXP, PILL), F32), ints, ints, ((9, C), F32)] + vectors,
         copies=True,
     )
-    got = exchange("pair_p", "pillars", part, None, peers, 2)
+    got = exchange("pair_p", "pillars", part, peers)
     ev = ((3 * C, NS * POS), BF16)
     od = ((3 * C, NS * (POS + OW)), BF16)
     z, part, *grid0 = call(
         first_conv_kernel, "conv0", [plane, rows8, ev, ev, od, od],
-        (got, hmax, cells, pfn_gain[None], pfn_bias[None], w),
+        (got, kept, w),
         [((GH * GW, PILL), BF16), ((2 * C, GH * GW), F32), buf],
     )
     pre = [z]
     stats = []
     for l in range(1, LAYERS):
-        got = exchange("pair_s", "stats", part, None, peers)
+        got = exchange("pair_s", "stats", part, peers)
         z, part, st = call(
-            conv_kernel, "conv", [plane, rows8, tile],
-            (jnp.full((1,), l, jnp.int32), got, pre[-1], bn_gain, bn_bias, w), [pad, pad, buf], scalar=True,
+            conv_kernel, f"conv{l}", [plane, rows8, tile], (got, pre[-1], kept, w), [pad, pad, buf], layer=l
         )
         pre.append(z)
         stats.append(st)
-    got = exchange("pair_s", "stats", part, part, peers)
+    got = exchange("pair_s", "stats", part, peers)
     slab = ((NS * C * OH, OW), F32)
-    payload = ((8 + 4 * BLOCK, 128), F32)
+    four = ((8 + 4 * BLOCK, 128), F32)
     feat, gy, keep, send, st = call(
-        turn_kernel, "turn", [slab, plane, payload, payload, tile],
-        (got, pre[-1], bn_gain, bn_bias, cotangent.reshape(NS * C * OH, OW), pre[0], stats[0], *grid0),
-        [buf],
+        turn_kernel, "turn", [slab, plane, four, four, tile],
+        (got, pre[-1], kept, cotangent.reshape(NS * C * OH, OW), pre[0], stats[0], *grid0), [buf],
     )
     stats.append(st)
     sums = [None] * LAYERS
-    reds = [None] * LAYERS
+    reds = []
     ends = []
-    blocks = 4
     for l in range(LAYERS - 1, 0, -1):
-        got = exchange(f"pair_g{blocks}", "sums", keep, send, peers, 1 + blocks * count, blocks * count)
-        after = 4 if l == 1 else 1
-        payload = ((8 + after * BLOCK, 128), F32)
-        gy, keep, send, sums[l], reds[l], *end_rows = call(
-            back_kernel, f"back{l}", [plane, payload, payload, row, ((blocks * count, 128), F32)] + [end] * (l > 1),
-            (got, pre[l], gy, stats[l], bn_gain, bn_bias, pre[l - 1], stats[l - 1], w)
-            + ((*grid0, *ends) if l == 1 else ()),
-            [pad, pad, pad, pad, plane, buf], layers=(l,), stride=1 + blocks * count,
+        got = exchange("pair_g", "sums", keep, peers, send)
+        blocks = got.shape[0] // peers - 1
+        fresh = ((8 + (3 if l == 1 else 1) * BLOCK, 128), F32)
+        gy, sums[l], red, keep, send, *last = call(
+            back_kernel, f"back{l}",
+            [plane, row, ((blocks, 128), F32), fresh, fresh] + [end] * (l > 1),
+            (got, pre[l], gy, stats[l], kept, pre[l - 1], stats[l - 1], w) + ((*grid0, *ends) if l == 1 else ()),
+            [pad, pad, pad, pad, plane, buf], layer=l, stride=blocks + 1,
         )
-        ends += end_rows
-        blocks = after
-    got = exchange(f"pair_g{blocks}", "sums", keep, send, peers, 1 + blocks * count, blocks * count)
+        reds.append(red)
+        ends += last
+    got = exchange("pair_z", "sums", keep, peers, send)
+    rows = (LAYERS + 1) * count
+    norm_grads, own, scales = call(
+        own_rows_kernel, "own_rows", [((2 * LAYERS, C), F32), ((peers * rows, 128), F32), ((3 * C, 128), F32)],
+        (got, stats[0], kept, *reds, *sums[1:]), stride=got.shape[0] // peers,
+    )
+    both = lax.all_gather(to_peers(own, peers), "k", tiled=True)
     tbuf = ((2 * C, POS + OW), BF16)
-    pillar_grad, norm_grads, own = call(
-        last_back_kernel, "back0",
-        [((NS * C, PILL), F32), ((2 * LAYERS, C), F32), (((LAYERS + 1) * count, 128), F32)],
-        (got, pre[0], gy, stats[0], bn_gain, bn_bias, cells, w, reds[3], reds[2], reds[1], *sums[1:]),
-        [tbuf, tbuf, ((2 * C, GH * GW), BF16), ((GH * GW, PILL), BF16), buf], stride=1 + blocks * count,
-    )
-    rows = (LAYERS + 1) * count
-    mine = to_peers(jnp.broadcast_to(own[None], (peers, rows, 128)).reshape(peers * rows, 128), peers)
+    (pillar_grad,) = call(
+        last_back_kernel, "back0", [((NS * C, PILL), F32)],
+        (pre[0], gy, stats[0], scales, kept, w),
+        [tbuf, tbuf, ((2 * C, GH * GW), BF16), ((GH * GW, PILL), BF16), buf],
+    )
     (total,) = call(
-        assemble_kernel, "assemble", [((9 * TAP_ROWS * LAYERS, 128), F32)], (mine, partner(mine)), peers=peers
+        assemble_kernel, "assemble", [((9 * TAP_ROWS * LAYERS, 128), F32)], (both,), peers=peers
     )
     total = total.reshape(9, TAP_ROWS, LAYERS, 128).transpose(2, 0, 1, 3).reshape(LAYERS, 9, C * C)
     return (

time: 256 us -> 249 us (0.973)
  blocking collectives: 201 us -> 188 us
  waiting for transfers between devices: 6.23 us -> 14.2 us
  local copies, waits for them, and re-layouts: 4.6 us -> 0.93 us
    all_to_all x10 -> x9, blocking collectives: 187 us -> 165 us  [to_peers(): return lax.all_to_all(sent, WIDE, 0, 0, tiled=True).reshape(-1, 128)]
    all_to_all x0 -> x1, waiting for transfers between devices: none -> 10.1 us  [to_peers(): return lax.all_to_all(sent, WIDE, 0, 0, tiled=True).reshape(-1, 128)]
    all_to_all x0 -> x1, starting transfers between devices: none -> 6.18 us  [to_peers(): return lax.all_to_all(sent, WIDE, 0, 0, tiled=True).reshape(-1, 128)]
    all_gather x0 -> x1, blocking collectives: none -> 5.3 us  [per_device(): both = lax.all_gather(to_peers(own, peers), 'k', tiled=True)]
    ppermute x6 -> x4, starting transfers between devices: 11.6 us -> 6.72 us  [partner(): return lax.ppermute(v, 'k', [(0, 1), (1, 0)])]
    unnamed x22 -> x8, local copies, waits for them, and re-layouts: 4.43 us -> 0.93 us
    all_gather x4 -> x5, blocking collectives: 13.9 us -> 17.4 us  [exchange(): lax.all_gather(keep, 'k', tiled=True)]
    ppermute x6 -> x4, waiting for transfers between devices: 6.23 us -> 4.06 us  [partner(): return lax.ppermute(v, 'k', [(0, 1), (1, 0)])]
  transfers between devices with their start and end apart: 6 -> 5, of which waited for: 6 -> 5; matrix products, arithmetic and copies ran while one was open for 0% -> 0% of each run, Pallas kernels for 0% -> 2%
where the time goes in v1:
time: 249 us; the launch traced here: 248 us
  blocking collectives  188 us (76%)
  Pallas kernels  31.9 us (13%)
  waiting for transfers between devices  14.2 us (6%)
  starting transfers between devices  12.9 us (5%)
    all_to_all x9, blocking collectives, to_peers(): return lax.all_to_all(sent, WIDE, 0, 0, tiled=True).reshape(-1, 128)  165 us
    pallas_call x21, Pallas kernels, call(): pl.pallas_call(functools.partial(kernel, **params) if params else kernel,...  31.9 us
    all_gather x5, blocking collectives, exchange(): lax.all_gather(keep, 'k', tiled=True)  17.4 us
    all_to_all x1, waiting for transfers between devices, to_peers(): return lax.all_to_all(sent, WIDE, 0, 0, tiled=True).reshape(-1, 128)  10.1 us
    ppermute x4, starting transfers between devices, partner(): return lax.ppermute(v, 'k', [(0, 1), (1, 0)])  6.72 us
    all_to_all x1, starting transfers between devices, to_peers(): return lax.all_to_all(sent, WIDE, 0, 0, tiled=True).reshape(-1, 128)  6.18 us
    all_gather x1, blocking collectives, per_device(): both = lax.all_gather(to_peers(own, peers), 'k', tiled=True)  5.3 us
  transfers between devices with their start and end apart: 5, of which 5 were waited for; matrix products, arithmetic and copies ran while one was open for 0% of the time, Pallas kernels for 2%

profile of v1, /device:TPU:1, one launch (start us, length us, event | category | flops | bytes accessed | tf_op | source)
XLA Modules:
  0.0 248.4 jit_solution(6396865290340540725)
XLA Ops:
  0.6 4.4 %pfn.1 = (f32[80,512]{1,0:T(8,128)}, f32[8,128]{1,0:T(8,128)}) custom-call(f32[256,256]{1,0:T(8,128)} %bitcast.82, s32[2,256]{1,0:T(2,128)} %cnt_in.1, s32[2,256]{1,0:T(2,128)} %cell_in.1, f32[9,64]{1,0:T(8,128)} %w_in.1, f32[4,64]{1,0:T(4,128)} %gain_in.1, f32[4,64]{1,0:T(4,128)} %bias_in.1, f32[1,64]{1,0:T(1,128)} %bitcast.84, f32[1,64]{1,0:T(1,128)} %bitcast.85), custom_call_target="tpu_custom_call" | custom-call | tf_op jit(solution)/shard_map/pfn/pallas_call | solution.py:700
  5.1 4.8 %all_gather.18.refs_0_ = f32[16,128]{1,0:T(8,128)S(1)} all-gather(f32[8,128]{1,0:T(8,128)} %get-tuple-element.46), channel_id=1, replica_groups=mesh['x'=4,'k'=2,'y'=4,'z'=8] {'k'}, dimensions={0}, use_global_device_ids=true | all-gather | bytes 12288 | tf_op jit(solution)/shard_map/all_gather | solution.py:722
  10.0 25.1 %all_to_all.50 = f32[128,2,1,128]{3,1,2,0:T(2,128)S(1)} all-to-all(f32[128,2,1,128]{3,1,2,0:T(2,128)S(1)} %bitcast.70), channel_id=1, replica_groups=mesh['x'=4,'k'=2,'y'=4,'z'=8] {'x','y','z'}, dimensions={0} | all-to-all | bytes 262144 | tf_op jit(solution)/shard_map/all_to_all | solution.py:718
  36.0 2.9 %conv0.1 = (f32[64,1024]{1,0:T(8,128)S(1)}, f32[8,128]{1,0:T(8,128)S(1)}, bf16[192,1024]{1,0:T(8,128)(2,1)S(1)}, bf16[192,1024]{1,0:T(8,128)(2,1)S(1)}, bf16[192...) custom-call(f32[256,128]{1,0:T(8,128)S(1)} %bitcast.67, f32[80,512]{1,0:T(8,128)S(1)} %copy-done.1, ...), custom_call_target="tpu_custom_call" | custom-call | tf_op jit(solution)/shard_map/conv0/pallas_call | solution.py:700
  38.9 3.3 %all_gather.19.refs_0_ = f32[16,128]{1,0:T(8,128)S(1)} all-gather(f32[8,128]{1,0:T(8,128)S(1)} %get-tuple-element.48), channel_id=1, replica_groups=mesh['x'=4,'k'=2,'y'=4,'z'=8] {'k'}, dimensions={0}, use_global_device_ids=true | all-gather | bytes 12288 | tf_op jit(solution)/shard_map/all_gather | solution.py:722
  42.3 16.1 %all_to_all.51 = f32[128,1,1,128]{3,2,1,0:T(1,128)S(1)} all-to-all(f32[128,1,1,128]{3,2,1,0:T(1,128)S(1)} %bitcast.75), channel_id=1, replica_groups=mesh['x'=4,'k'=2,'y'=4,'z'=8] {'x','y','z'}, dimensions={0} | all-to-all | bytes 131072 | tf_op jit(solution)/shard_map/all_to_all | solution.py:718
  60.1 3.1 %all_gather.20.refs_0_ = f32[16,128]{1,0:T(8,128)S(1)} all-gather(f32[8,128]{1,0:T(8,128)S(1)} %get-tuple-element.50), channel_id=1, replica_groups=mesh['x'=4,'k'=2,'y'=4,'z'=8] {'k'}, dimensions={0}, use_global_device_ids=true | all-gather | bytes 12288 | tf_op jit(solution)/shard_map/all_gather | solution.py:722
  63.2 16.1 %all_to_all.52 = f32[128,1,1,128]{3,2,1,0:T(1,128)S(1)} all-to-all(f32[128,1,1,128]{3,2,1,0:T(1,128)S(1)} %bitcast.76), channel_id=1, replica_groups=mesh['x'=4,'k'=2,'y'=4,'z'=8] {'x','y','z'}, dimensions={0} | all-to-all | bytes 131072 | tf_op jit(solution)/shard_map/all_to_all | solution.py:718
  81.0 3.0 %all_gather.21.refs_0_ = f32[16,128]{1,0:T(8,128)S(1)} all-gather(f32[8,128]{1,0:T(8,128)S(1)} %get-tuple-element.52), channel_id=1, replica_groups=mesh['x'=4,'k'=2,'y'=4,'z'=8] {'k'}, dimensions={0}, use_global_device_ids=true | all-gather | bytes 12288 | tf_op jit(solution)/shard_map/all_gather | solution.py:722
  84.1 16.1 %all_to_all.53 = f32[128,1,1,128]{3,2,1,0:T(1,128)S(1)} all-to-all(f32[128,1,1,128]{3,2,1,0:T(1,128)S(1)} %bitcast.77), channel_id=1, replica_groups=mesh['x'=4,'k'=2,'y'=4,'z'=8] {'x','y','z'}, dimensions={0} | all-to-all | bytes 131072 | tf_op jit(solution)/shard_map/all_to_all | solution.py:718
  101.8 3.2 %all_gather.22.refs_0_ = f32[16,128]{1,0:T(8,128)S(1)} all-gather(f32[8,128]{1,0:T(8,128)S(1)} %get-tuple-element.54), channel_id=1, replica_groups=mesh['x'=4,'k'=2,'y'=4,'z'=8] {'k'}, dimensions={0}, use_global_device_ids=true | all-gather | bytes 12288 | tf_op jit(solution)/shard_map/all_gather | solution.py:722
  105.1 16.1 %all_to_all.54 = f32[128,1,1,128]{3,2,1,0:T(1,128)S(1)} all-to-all(f32[128,1,1,128]{3,2,1,0:T(1,128)S(1)} %bitcast.78), channel_id=1, replica_groups=mesh['x'=4,'k'=2,'y'=4,'z'=8] {'x','y','z'}, dimensions={0} | all-to-all | bytes 131072 | tf_op jit(solution)/shard_map/all_to_all | solution.py:718
  121.2 3.1 %turn.1 = (f32[512,128]{1,0:T(8,128)}, f32[64,1024]{1,0:T(8,128)S(1)}, f32[520,128]{1,0:T(8,128)S(1)}, f32[520,128]{1,0:T(8,128)S(1)}, f32[128,128]{1,0:T(8,128)S(1)}) custom-call(f32[128,128]{1,0:T(8,128)S(1)} %bitcast.71, f32[64,1024]{1,0:T(8,128)S(1)} %get-tuple-element.55.z_ref, f32[80,512]{1,0:T(8,128)S(1)} %copy-done.2, f32[512,128]{1,0:T(8,128)S(1)} %bitcast.79, ...), custom_call_target="tpu_custom_call" | custom-call | tf_op jit(solution)/shard_map/turn/pallas_call | solution.py:700
  127.1 21.0 %all_to_all.55 = f32[128,5,1,128]{3,2,1,0:T(1,128)S(1)} all-to-all(f32[128,5,1,128]{3,2,1,0:T(1,128)S(1)} %bitcast.61), channel_id=1, replica_groups=mesh['x'=4,'k'=2,'y'=4,'z'=8] {'x','y','z'}, dimensions={0} | all-to-all | bytes 655360 | tf_op jit(solution)/shard_map/all_to_all | solution.py:718
  148.1 3.1 %back3.1 = (f32[64,1024]{1,0:T(8,128)S(1)}, f32[1,128]{1,0:T(1,128)S(1)}, f32[4,128]{1,0:T(4,128)S(1)}, f32[136,128]{1,0:T(8,128)S(1)}, f32[136,128]{1,0:T(8,128)S(1)}, /*index=5*/f32[32,128]{1,0:T(8,128)S(1)}) custom-call(f32[640,128]{1,0:T(8,128)S(1)} %bitcast.62, f32[64,1024]{1,0:T(8,128)S(1)} %get-tuple-element.55.z_ref, ...), custom_call_target="tpu_custom_call" | custom-call | tf_op jit(solution)/shard_map/back3/pallas_call | solution.py:700
  154.1 17.3 %all_to_all.56 = f32[128,2,1,128]{3,1,2,0:T(2,128)S(1)} all-to-all(f32[128,2,1,128]{3,1,2,0:T(2,128)S(1)} %bitcast.68), channel_id=1, replica_groups=mesh['x'=4,'k'=2,'y'=4,'z'=8] {'x','y','z'}, dimensions={0} | all-to-all | bytes 262144 | tf_op jit(solution)/shard_map/all_to_all | solution.py:718
  171.4 3.1 %back2.1 = (f32[64,1024]{1,0:T(8,128)S(1)}, f32[1,128]{1,0:T(1,128)S(1)}, f32[1,128]{1,0:T(1,128)S(1)}, f32[136,128]{1,0:T(8,128)S(1)}, f32[136,128]{1,0:T(8,128)S(1)}, /*index=5*/f32[32,128]{1,0:T(8,128)S(1)}) custom-call(f32[256,128]{1,0:T(8,128)S(1)} %bitcast.66, f32[64,1024]{1,0:T(8,128)S(1)} %get-tuple-element.53.z_ref.zp_ref, ...), custom_call_target="tpu_custom_call" | custom-call | tf_op jit(solution)/shard_map/back2/pallas_call | solution.py:700
  176.9 17.4 %all_to_all.57 = f32[128,2,1,128]{3,1,2,0:T(2,128)S(1)} all-to-all(f32[128,2,1,128]{3,1,2,0:T(2,128)S(1)} %bitcast.69), channel_id=1, replica_groups=mesh['x'=4,'k'=2,'y'=4,'z'=8] {'x','y','z'}, dimensions={0} | all-to-all | bytes 262144 | tf_op jit(solution)/shard_map/all_to_all | solution.py:718
  194.3 4.3 %back1.1 = (f32[64,1024]{1,0:T(8,128)S(1)}, f32[1,128]{1,0:T(1,128)S(1)}, f32[1,128]{1,0:T(1,128)S(1)}, f32[392,128]{1,0:T(8,128)S(1)}, f32[392,128]{1,0:T(8,128)S(1)}) custom-call(f32[256,128]{1,0:T(8,128)S(1)} %bitcast.65, f32[64,1024]{1,0:T(8,128)S(1)} %get-tuple-element.51.z_ref.zp_ref, f32[64,1024]{1,0:T(8,128)S(1)} %get-tuple-element.73.gy_ref, ...), custom_call_target="tpu_custom_call" | custom-call | tf_op jit(solution)/shard_map/back1/pallas_call | solution.py:700
  201.3 19.8 %all_to_all.58 = f32[128,4,1,128]{3,1,2,0:T(4,128)S(1)} all-to-all(f32[128,4,1,128]{3,1,2,0:T(4,128)S(1)} %bitcast.64), channel_id=1, replica_groups=mesh['x'=4,'k'=2,'y'=4,'z'=8] {'x','y','z'}, dimensions={0} | all-to-all | bytes 524288 | tf_op jit(solution)/shard_map/all_to_all | solution.py:718
  222.0 6.2 %all-to-all-start.9 = ((f32[128,5,1,128]{3,2,1,0:T(1,128)}), f32[128,5,1,128]{3,2,1,0:T(1,128)S(1)}, u32[]{:S(2)}, u32[]{:S(2)}) async-start(f32[128,5,1,128]{3,2,1,0:T(1,128)} %bitcast.36), calls=%async_computation.9 | async-start | bytes 655360 | tf_op jit(solution)/shard_map/all_to_all | solution.py:718
  228.2 3.9 %back0.1 = f32[128,256]{1,0:T(8,128)} custom-call(f32[64,1024]{1,0:T(8,128)S(1)} %get-tuple-element.49.z_ref.z0_ref.zp_ref, f32[64,1024]{1,0:T(8,128)S(1)} %get-tuple-element.86.gy_ref, f32[128,128]{1,0:T(8,128)S(1)} %get-tuple-element.56.stats0_ref.statsp_ref.stats_ref, f32[192,128]{1,0:T(8,128)S(1)} %get-tuple-element.87.scale_ref, ...), custom_call_target="tpu_custom_call" | custom-call | tf_op jit(solution)/shard_map/back0/pallas_call | solution.py:700
  232.1 10.1 %all-to-all-done.9 = f32[128,5,1,128]{3,2,1,0:T(1,128)S(1)} async-done(((f32[128,5,1,128]{3,2,1,0:T(1,128)}), f32[128,5,1,128]{3,2,1,0:T(1,128)S(1)}, u32[]{:S(2)}, u32[]{:S(2)}) %all-to-all-start.9) | async-done | bytes 327712 | tf_op jit(solution)/shard_map/all_to_all | solution.py:718
  242.2 5.3 %all_gather.23.both_ref = f32[1280,128]{1,0:T(8,128)S(1)} all-gather(f32[640,128]{1,0:T(8,128)S(1)} %bitcast.80), channel_id=1, replica_groups=mesh['x'=4,'k'=2,'y'=4,'z'=8] {'k'}, dimensions={0}, use_global_device_ids=true | all-gather | bytes 983040 | tf_op jit(solution)/shard_map/all_gather | solution.py:800
  (30 shorter events, 18.9 us)
Async XLA Ops:
  0.6 34.5 %copy-start = (f32[4,9,4096]{2,0,1:T(4,128)S(1)}, f32[4,9,4096]{2,0,1:T(4,128)}, u32[]{:S(2)}) copy-start(f32[4,9,4096]{2,0,1:T(4,128)} %param.16) | copy-start | bytes 1769476
  35.1 0.9 copy-start.1
  38.9 19.5 %copy-start.2 = (f32[80,512]{1,0:T(8,128)S(1)}, f32[80,512]{1,0:T(8,128)}, u32[]{:S(2)}) copy-start(f32[80,512]{1,0:T(8,128)} %get-tuple-element.47.kept_ref.gb_ref) | copy-start | bytes 491524
  100.2 21.0 %copy-start.3 = (f32[2,64,4,128]{3,2,1,0:T(4,128)S(1)}, f32[2,64,4,128]{3,2,1,0:T(4,128)}, u32[]{:S(2)}) copy-start(f32[2,64,4,128]{3,2,1,0:T(4,128)} %param.19) | copy-start | bytes 786436
  124.3 2.7 %collective-permute-start = (f32[520,128]{1,0:T(8,128)S(1)}, f32[520,128]{1,0:T(8,128)S(1)}, u32[]{:S(2)}, u32[]{:S(2)}) collective-permute-start(f32[520,128]{1,0:T(8,128)S(1)} %get-tuple-element.63), channel_id=1, source_target_pairs={{0,32},{32,0},{1,33},{33,1},{2,34},{34,2},{3,35},{35,3},{4,36},{36... | collective-permute-start | bytes 798728 | tf_op jit(solution)/shard_map/ppermute | solution.py:713
  151.2 2.9 %collective-permute-start.1 = (f32[136,128]{1,0:T(8,128)S(1)}, f32[136,128]{1,0:T(8,128)S(1)}, u32[]{:S(2)}, u32[]{:S(2)}) collective-permute-start(f32[136,128]{1,0:T(8,128)S(1)} %get-tuple-element.68), channel_id=1, source_target_pairs={{0,32},{32,0},{1,33},{33,1},{2,34},{34,2},{3,35},{35,3},{4,36},{36... | collective-permute-start | bytes 208904 | tf_op jit(solution)/shard_map/ppermute | solution.py:713
  174.4 2.5 collective-permute-start.2
  198.6 2.7 %collective-permute-start.3 = (f32[392,128]{1,0:T(8,128)S(1)}, f32[392,128]{1,0:T(8,128)S(1)}, u32[]{:S(2)}, u32[]{:S(2)}) collective-permute-start(f32[392,128]{1,0:T(8,128)S(1)} %get-tuple-element.77), channel_id=1, source_target_pairs={{0,32},{32,0},{1,33},{33,1},{2,34},{34,2},{3,35},{35,3},{4,36},{36... | collective-permute-start | bytes 602120 | tf_op jit(solution)/shard_map/ppermute | solution.py:713
  222.0 20.2 %all-to-all-start.9 = ((f32[128,5,1,128]{3,2,1,0:T(1,128)}), f32[128,5,1,128]{3,2,1,0:T(1,128)S(1)}, u32[]{:S(2)}, u32[]{:S(2)}) async-start(f32[128,5,1,128]{3,2,1,0:T(1,128)} %bitcast.36), calls=%async_computation.9 | async-start | bytes 655360 | tf_op jit(solution)/shard_map/all_to_all | solution.py:718

commit v2 on v1

--- a/solution.py
+++ b/solution.py
@@ -392,11 +392,14 @@
     store_stats(z_ref, part_ref)
 
 
-def first_grad_rows(grad_of, grid_refs):
+def first_grad_rows(grad_of, grid_refs, extra=0):
     ev_hi, ev_lo, od_hi, od_lo = grid_refs
+    ones = [jnp.ones((extra, POS), BF16)] * (extra > 0)
 
     def sweep(n, rows):
         g_hi, g_lo = grad_of(n)
+        whole = jnp.concatenate([g_hi, g_lo, *ones], axis=0)
+        upper = jnp.concatenate([g_hi, *ones], axis=0) if extra else g_hi
         out = []
         for row, hi, lo, start in zip(
             rows,
@@ -405,30 +408,12 @@
             (n * (POS + OW), n * POS, n * (POS + OW) + OW),
         ):
             at = lanes_from(start, POS)
-            out.append(row + dot3(dot_nt, g_hi, g_lo, hi[:, at], lo[:, at]))
+            high = dot_nt(whole, hi[:, at])
+            both = jnp.concatenate([high[:C] + high[C : 2 * C], high[2 * C :]], axis=0) if extra else high[:C] + high[C:]
+            out.append(row + both + dot_nt(upper, lo[:, at]))
         return tuple(out)
 
-    return each_sweep(sweep, tuple(jnp.zeros((C, 3 * C), F32) for _ in range(3)))
-
-
-def first_input_sums(grid_refs):
-    ev_hi, ev_lo, od_hi, od_lo = grid_refs
-    one = jnp.ones((16, POS), BF16)
-
-    def sweep(n, rows):
-        out = []
-        for row, hi, lo, start in zip(
-            rows,
-            (od_hi, ev_hi, od_hi),
-            (od_lo, ev_lo, od_lo),
-            (n * (POS + OW), n * POS, n * (POS + OW) + OW),
-        ):
-            at = lanes_from(start, POS)
-            out.append(row + dot_nt(one, hi[:, at]) + dot_nt(one, lo[:, at]))
-        return tuple(out)
-
-    rows = each_sweep(sweep, tuple(jnp.zeros((16, 3 * C), F32) for _ in range(3)))
-    return [jnp.broadcast_to(row[:1], (C, 3 * C)) for row in rows]
+    return each_sweep(sweep, tuple(jnp.zeros((C + extra, 3 * C), F32) for _ in range(3)))
 
 
 def conv_kernel(
@@ -483,15 +468,14 @@
     send_ref[pl.ds(0, 1), :] = part
     mean0, inv0 = stats0_ref[pl.ds(0, C), pl.ds(0, 1)], stats0_ref[pl.ds(C, C), pl.ds(0, 1)]
     grads = first_grad_rows(
-        lambda n: split((z0_ref[:, lanes_from(n * POS, POS)] - mean0) * inv0), (ev_hi, ev_lo, od_hi, od_lo)
+        lambda n: split((z0_ref[:, lanes_from(n * POS, POS)] - mean0) * inv0), (ev_hi, ev_lo, od_hi, od_lo), 16
     )
     refs = (keep_ref, send_ref)
     none = jnp.zeros((TAP_ROWS, 128), F32)
-    last = store_kernel_grad(refs, 0, grads, buf_ref)
-    store_half(refs, 2, [last, none, none, none], [none] * 4)
-    grads = first_input_sums((ev_hi, ev_lo, od_hi, od_lo))
-    last = store_kernel_grad(refs, 1, grads, buf_ref)
-    store_half(refs, 3, [last, none, none, none], [none] * 4)
+    last = store_kernel_grad(refs, 0, [row[:C] for row in grads], buf_ref)
+    sums = [jnp.broadcast_to(row[C : C + 1], (C, 3 * C)) for row in grads]
+    last_sums = store_kernel_grad(refs, 1, sums, buf_ref)
+    store_half(refs, 2, [last, last_sums, none, none], [none] * 4)
 
 
 def grad_scales(g, stats, gain):
@@ -600,8 +584,12 @@
         here, raw, ends = (
             jnp.sum(rows_of(g_ref, stride, 1 + q * count + j), axis=0, keepdims=True) for q in range(3)
         )
-        normed, plain, normed_end, plain_end = (first_red[pl.ds(q * count + j, 1), :] for q in range(4))
-        ends = jnp.where(first_core(), first_grad(ends, normed_end, plain_end, pair), ends)
+        normed, plain, end = (first_red[pl.ds(q * count + j, 1), :] for q in range(3))
+        plain_peer = lax.div(j * peers + spot, TAP_ROWS) == 1
+        end_grad = pick_channels(scale, pair, lane) * (
+            ends - pick_channels(jnp.where(plain_peer, mean_dy, mean_dx), pair, lane) * end
+        )
+        ends = jnp.where(first_core(), end_grad, ends)
         own = (first_grad(raw, normed, plain, pair), here, red2[pl.ds(j, 1), :], red3[pl.ds(j, 1), :], ends)
         for q in range(5):
             at = pl.ds(q * count + j, peers, stride=5 * count)
@@ -692,6 +680,9 @@
         for step in range(0, TAP_ROWS, size):
             start = max(l - 1, 0) * TAP_ROWS + step
             rows = rows_at(min(l, 1), start % peers * per_peer + LAYERS * count + start // peers, size)
+            if l == 0:
+                start += TAP_ROWS
+                rows = rows + rows_at(0, start % peers * per_peer + LAYERS * count + start // peers, size)
             out_ref[pl.ds((2 * BLOCK + step) * LAYERS + l, size, stride=LAYERS), :] = rows
 
 
@@ -762,7 +753,7 @@
     pre = [z]
     stats = []
     for l in range(1, LAYERS):
-        got = exchange("pair_s", "stats", part, peers)
+        got = exchange("pair_s", "stats", part, peers, part if l == 1 else None)
         z, part, st = call(
             conv_kernel, f"conv{l}", [plane, rows8, tile], (got, pre[-1], kept, w), [pad, pad, buf], layer=l
         )
@@ -770,9 +761,9 @@
         stats.append(st)
     got = exchange("pair_s", "stats", part, peers)
     slab = ((NS * C * OH, OW), F32)
-    four = ((8 + 4 * BLOCK, 128), F32)
+    three = ((8 + 3 * BLOCK, 128), F32)
     feat, gy, keep, send, st = call(
-        turn_kernel, "turn", [slab, plane, four, four, tile],
+        turn_kernel, "turn", [slab, plane, three, three, tile],
         (got, pre[-1], kept, cotangent.reshape(NS * C * OH, OW), pre[0], stats[0], *grid0), [buf],
     )
     stats.append(st)

time: 249 us -> 246 us (0.988)
  blocking collectives: 188 us -> 183 us
    all_gather x5 -> x4, blocking collectives: 17.4 us -> 13.9 us  [exchange(): lax.all_gather(keep, 'k', tiled=True)]
    ppermute x4 -> x5, starting transfers between devices: 6.72 us -> 8.51 us  [partner(): return lax.ppermute(v, 'k', [(0, 1), (1, 0)])]
  transfers between devices with their start and end apart: 5 -> 6, of which waited for: 5 -> 6; matrix products, arithmetic and copies ran while one was open for 0% -> 0% of each run, Pallas kernels for 2% -> 2%
where the time goes in v2:
time: 246 us; the launch traced here: 245 us
  blocking collectives  183 us (74%)
  Pallas kernels  31.2 us (13%)
  waiting for transfers between devices  14.9 us (6%)
  starting transfers between devices  14.7 us (6%)
    all_to_all x9, blocking collectives, to_peers(): return lax.all_to_all(sent, WIDE, 0, 0, tiled=True).reshape(-1, 128)  164 us
    pallas_call x21, Pallas kernels, call(): pl.pallas_call(functools.partial(kernel, **params) if params else kernel,...  31.2 us
    all_gather x4, blocking collectives, exchange(): lax.all_gather(keep, 'k', tiled=True)  13.9 us
    all_to_all x1, waiting for transfers between devices, to_peers(): return lax.all_to_all(sent, WIDE, 0, 0, tiled=True).reshape(-1, 128)  10.1 us
    ppermute x5, starting transfers between devices, partner(): return lax.ppermute(v, 'k', [(0, 1), (1, 0)])  8.51 us
    all_to_all x1, starting transfers between devices, to_peers(): return lax.all_to_all(sent, WIDE, 0, 0, tiled=True).reshape(-1, 128)  6.18 us
    all_gather x1, blocking collectives, per_device(): both = lax.all_gather(to_peers(own, peers), 'k', tiled=True)  5.3 us
  transfers between devices with their start and end apart: 6, of which 6 were waited for; matrix products, arithmetic and copies ran while one was open for 0% of the time, Pallas kernels for 2%

profile of v2, /device:TPU:1, one launch (start us, length us, event | category | flops | bytes accessed | tf_op | source)
XLA Modules:
  0.0 245.4 jit_solution(8384364105814957886)
XLA Ops:
  0.6 4.4 %pfn.1 = (f32[80,512]{1,0:T(8,128)}, f32[8,128]{1,0:T(8,128)}) custom-call(f32[256,256]{1,0:T(8,128)} %bitcast.84, s32[2,256]{1,0:T(2,128)} %cnt_in.1, s32[2,256]{1,0:T(2,128)} %cell_in.1, f32[9,64]{1,0:T(8,128)} %w_in.1, f32[4,64]{1,0:T(4,128)} %gain_in.1, f32[4,64]{1,0:T(4,128)} %bias_in.1, f32[1,64]{1,0:T(1,128)} %bitcast.86, f32[1,64]{1,0:T(1,128)} %bitcast.87), custom_call_target="tpu_custom_call" | custom-call | tf_op jit(solution)/shard_map/pfn/pallas_call | solution.py:691
  5.1 4.8 %all_gather.15.refs_0_ = f32[16,128]{1,0:T(8,128)S(1)} all-gather(f32[8,128]{1,0:T(8,128)} %get-tuple-element.46), channel_id=1, replica_groups=mesh['x'=4,'k'=2,'y'=4,'z'=8] {'k'}, dimensions={0}, use_global_device_ids=true | all-gather | bytes 12288 | tf_op jit(solution)/shard_map/all_gather | solution.py:713
  10.0 25.1 %all_to_all.50 = f32[128,2,1,128]{3,1,2,0:T(2,128)S(1)} all-to-all(f32[128,2,1,128]{3,1,2,0:T(2,128)S(1)} %bitcast.72), channel_id=1, replica_groups=mesh['x'=4,'k'=2,'y'=4,'z'=8] {'x','y','z'}, dimensions={0} | all-to-all | bytes 262144 | tf_op jit(solution)/shard_map/all_to_all | solution.py:709
  36.0 2.9 %conv0.1 = (f32[64,1024]{1,0:T(8,128)S(1)}, f32[8,128]{1,0:T(8,128)S(1)}, bf16[192,1024]{1,0:T(8,128)(2,1)S(1)}, bf16[192,1024]{1,0:T(8,128)(2,1)S(1)}, bf16[192...) custom-call(f32[256,128]{1,0:T(8,128)S(1)} %bitcast.69, f32[80,512]{1,0:T(8,128)S(1)} %copy-done.1, ...), custom_call_target="tpu_custom_call" | custom-call | tf_op jit(solution)/shard_map/conv0/pallas_call | solution.py:691
  41.6 16.1 %all_to_all.51 = f32[128,1,1,128]{3,2,1,0:T(1,128)S(1)} all-to-all(f32[128,1,1,128]{3,2,1,0:T(1,128)S(1)} %bitcast.77), channel_id=1, replica_groups=mesh['x'=4,'k'=2,'y'=4,'z'=8] {'x','y','z'}, dimensions={0} | all-to-all | bytes 131072 | tf_op jit(solution)/shard_map/all_to_all | solution.py:709
  59.4 3.1 %all_gather.16.refs_0_ = f32[16,128]{1,0:T(8,128)S(1)} all-gather(f32[8,128]{1,0:T(8,128)S(1)} %get-tuple-element.50), channel_id=1, replica_groups=mesh['x'=4,'k'=2,'y'=4,'z'=8] {'k'}, dimensions={0}, use_global_device_ids=true | all-gather | bytes 12288 | tf_op jit(solution)/shard_map/all_gather | solution.py:713
  62.5 16.1 %all_to_all.52 = f32[128,1,1,128]{3,2,1,0:T(1,128)S(1)} all-to-all(f32[128,1,1,128]{3,2,1,0:T(1,128)S(1)} %bitcast.78), channel_id=1, replica_groups=mesh['x'=4,'k'=2,'y'=4,'z'=8] {'x','y','z'}, dimensions={0} | all-to-all | bytes 131072 | tf_op jit(solution)/shard_map/all_to_all | solution.py:709
  80.3 3.0 %all_gather.17.refs_0_ = f32[16,128]{1,0:T(8,128)S(1)} all-gather(f32[8,128]{1,0:T(8,128)S(1)} %get-tuple-element.52), channel_id=1, replica_groups=mesh['x'=4,'k'=2,'y'=4,'z'=8] {'k'}, dimensions={0}, use_global_device_ids=true | all-gather | bytes 12288 | tf_op jit(solution)/shard_map/all_gather | solution.py:713
  83.4 16.1 %all_to_all.53 = f32[128,1,1,128]{3,2,1,0:T(1,128)S(1)} all-to-all(f32[128,1,1,128]{3,2,1,0:T(1,128)S(1)} %bitcast.79), channel_id=1, replica_groups=mesh['x'=4,'k'=2,'y'=4,'z'=8] {'x','y','z'}, dimensions={0} | all-to-all | bytes 131072 | tf_op jit(solution)/shard_map/all_to_all | solution.py:709
  101.1 3.0 %all_gather.18.refs_0_ = f32[16,128]{1,0:T(8,128)S(1)} all-gather(f32[8,128]{1,0:T(8,128)S(1)} %get-tuple-element.54), channel_id=1, replica_groups=mesh['x'=4,'k'=2,'y'=4,'z'=8] {'k'}, dimensions={0}, use_global_device_ids=true | all-gather | bytes 12288 | tf_op jit(solution)/shard_map/all_gather | solution.py:713
  104.3 16.1 %all_to_all.54 = f32[128,1,1,128]{3,2,1,0:T(1,128)S(1)} all-to-all(f32[128,1,1,128]{3,2,1,0:T(1,128)S(1)} %bitcast.80), channel_id=1, replica_groups=mesh['x'=4,'k'=2,'y'=4,'z'=8] {'x','y','z'}, dimensions={0} | all-to-all | bytes 131072 | tf_op jit(solution)/shard_map/all_to_all | solution.py:709
  120.4 2.4 turn.1
  125.4 19.9 %all_to_all.55 = f32[128,4,1,128]{3,1,2,0:T(4,128)S(1)} all-to-all(f32[128,4,1,128]{3,1,2,0:T(4,128)S(1)} %bitcast.64), channel_id=1, replica_groups=mesh['x'=4,'k'=2,'y'=4,'z'=8] {'x','y','z'}, dimensions={0} | all-to-all | bytes 524288 | tf_op jit(solution)/shard_map/all_to_all | solution.py:709
  145.3 3.1 %back3.1 = (f32[64,1024]{1,0:T(8,128)S(1)}, f32[1,128]{1,0:T(1,128)S(1)}, f32[3,128]{1,0:T(4,128)S(1)}, f32[136,128]{1,0:T(8,128)S(1)}, f32[136,128]{1,0:T(8,128)S(1)}, /*index=5*/f32[32,128]{1,0:T(8,128)S(1)}) custom-call(f32[512,128]{1,0:T(8,128)S(1)} %bitcast.66, f32[64,1024]{1,0:T(8,128)S(1)} %get-tuple-element.55.z_ref, ...), custom_call_target="tpu_custom_call" | custom-call | tf_op jit(solution)/shard_map/back3/pallas_call | solution.py:691
  151.0 17.3 %all_to_all.56 = f32[128,2,1,128]{3,1,2,0:T(2,128)S(1)} all-to-all(f32[128,2,1,128]{3,1,2,0:T(2,128)S(1)} %bitcast.70), channel_id=1, replica_groups=mesh['x'=4,'k'=2,'y'=4,'z'=8] {'x','y','z'}, dimensions={0} | all-to-all | bytes 262144 | tf_op jit(solution)/shard_map/all_to_all | solution.py:709
  168.3 3.0 %back2.1 = (f32[64,1024]{1,0:T(8,128)S(1)}, f32[1,128]{1,0:T(1,128)S(1)}, f32[1,128]{1,0:T(1,128)S(1)}, f32[136,128]{1,0:T(8,128)S(1)}, f32[136,128]{1,0:T(8,128)S(1)}, /*index=5*/f32[32,128]{1,0:T(8,128)S(1)}) custom-call(f32[256,128]{1,0:T(8,128)S(1)} %bitcast.68, f32[64,1024]{1,0:T(8,128)S(1)} %get-tuple-element.53.z_ref.zp_ref, ...), custom_call_target="tpu_custom_call" | custom-call | tf_op jit(solution)/shard_map/back2/pallas_call | solution.py:691
  171.3 1.8 collective-permute-start.3
  174.1 17.2 %all_to_all.57 = f32[128,2,1,128]{3,1,2,0:T(2,128)S(1)} all-to-all(f32[128,2,1,128]{3,1,2,0:T(2,128)S(1)} %bitcast.71), channel_id=1, replica_groups=mesh['x'=4,'k'=2,'y'=4,'z'=8] {'x','y','z'}, dimensions={0} | all-to-all | bytes 262144 | tf_op jit(solution)/shard_map/all_to_all | solution.py:709
  191.2 4.3 %back1.1 = (f32[64,1024]{1,0:T(8,128)S(1)}, f32[1,128]{1,0:T(1,128)S(1)}, f32[1,128]{1,0:T(1,128)S(1)}, f32[392,128]{1,0:T(8,128)S(1)}, f32[392,128]{1,0:T(8,128)S(1)}) custom-call(f32[256,128]{1,0:T(8,128)S(1)} %bitcast.67, f32[64,1024]{1,0:T(8,128)S(1)} %get-tuple-element.51.z_ref.zp_ref, f32[64,1024]{1,0:T(8,128)S(1)} %get-tuple-element.73.gy_ref, ...), custom_call_target="tpu_custom_call" | custom-call | tf_op jit(solution)/shard_map/back1/pallas_call | solution.py:691
  198.3 19.8 %all_to_all.58 = f32[128,4,1,128]{3,1,2,0:T(4,128)S(1)} all-to-all(f32[128,4,1,128]{3,1,2,0:T(4,128)S(1)} %bitcast.65), channel_id=1, replica_groups=mesh['x'=4,'k'=2,'y'=4,'z'=8] {'x','y','z'}, dimensions={0} | all-to-all | bytes 524288 | tf_op jit(solution)/shard_map/all_to_all | solution.py:709
  219.0 6.2 %all-to-all-start.9 = ((f32[128,5,1,128]{3,2,1,0:T(1,128)}), f32[128,5,1,128]{3,2,1,0:T(1,128)S(1)}, u32[]{:S(2)}, u32[]{:S(2)}) async-start(f32[128,5,1,128]{3,2,1,0:T(1,128)} %bitcast.37), calls=%async_computation.9 | async-start | bytes 655360 | tf_op jit(solution)/shard_map/all_to_all | solution.py:709
  225.2 3.9 %back0.1 = f32[128,256]{1,0:T(8,128)} custom-call(f32[64,1024]{1,0:T(8,128)S(1)} %get-tuple-element.49.z_ref.z0_ref.zp_ref, f32[64,1024]{1,0:T(8,128)S(1)} %get-tuple-element.86.gy_ref, f32[128,128]{1,0:T(8,128)S(1)} %get-tuple-element.56.stats0_ref.statsp_ref.stats_ref, f32[192,128]{1,0:T(8,128)S(1)} %get-tuple-element.87.scale_ref, ...), custom_call_target="tpu_custom_call" | custom-call | tf_op jit(solution)/shard_map/back0/pallas_call | solution.py:691
  229.1 10.1 %all-to-all-done.9 = f32[128,5,1,128]{3,2,1,0:T(1,128)S(1)} async-done(((f32[128,5,1,128]{3,2,1,0:T(1,128)}), f32[128,5,1,128]{3,2,1,0:T(1,128)S(1)}, u32[]{:S(2)}, u32[]{:S(2)}) %all-to-all-start.9) | async-done | bytes 327712 | tf_op jit(solution)/shard_map/all_to_all | solution.py:709
  239.2 5.3 %all_gather.19.both_ref = f32[1280,128]{1,0:T(8,128)S(1)} all-gather(f32[640,128]{1,0:T(8,128)S(1)} %bitcast.82), channel_id=1, replica_groups=mesh['x'=4,'k'=2,'y'=4,'z'=8] {'k'}, dimensions={0}, use_global_device_ids=true | all-gather | bytes 983040 | tf_op jit(solution)/shard_map/all_gather | solution.py:791
  (31 shorter events, 19.6 us)
Async XLA Ops:
  0.6 34.5 %copy-start = (f32[4,9,4096]{2,0,1:T(4,128)S(1)}, f32[4,9,4096]{2,0,1:T(4,128)}, u32[]{:S(2)}) copy-start(f32[4,9,4096]{2,0,1:T(4,128)} %param.16) | copy-start | bytes 1769476
  35.1 0.9 copy-start.1
  38.9 18.8 %copy-start.2 = (f32[80,512]{1,0:T(8,128)S(1)}, f32[80,512]{1,0:T(8,128)}, u32[]{:S(2)}) copy-start(f32[80,512]{1,0:T(8,128)} %get-tuple-element.47.kept_ref.gb_ref) | copy-start | bytes 491524
  38.9 2.6 %collective-permute-start = (f32[8,128]{1,0:T(8,128)S(1)}, f32[8,128]{1,0:T(8,128)S(1)}, u32[]{:S(2)}, u32[]{:S(2)}) collective-permute-start(f32[8,128]{1,0:T(8,128)S(1)} %get-tuple-element.48.refs_0_), channel_id=1, source_target_pairs={{0,32},{32,0},{1,33},{33,1},{2,34},{34,2},{3,35},{35,3},{4,36},{36... | collective-permute-start | bytes 12296 | tf_op jit(solution)/shard_map/ppermute | solution.py:704
  99.5 20.9 %copy-start.3 = (f32[2,64,4,128]{3,2,1,0:T(4,128)S(1)}, f32[2,64,4,128]{3,2,1,0:T(4,128)}, u32[]{:S(2)}) copy-start(f32[2,64,4,128]{3,2,1,0:T(4,128)} %param.19) | copy-start | bytes 786436
  122.7 2.7 %collective-permute-start.1 = (f32[392,128]{1,0:T(8,128)S(1)}, f32[392,128]{1,0:T(8,128)S(1)}, u32[]{:S(2)}, u32[]{:S(2)}) collective-permute-start(f32[392,128]{1,0:T(8,128)S(1)} %get-tuple-element.63), channel_id=1, source_target_pairs={{0,32},{32,0},{1,33},{33,1},{2,34},{34,2},{3,35},{35,3},{4,36},{36... | collective-permute-start | bytes 602120 | tf_op jit(solution)/shard_map/ppermute | solution.py:704
  148.4 2.6 %collective-permute-start.2 = (f32[136,128]{1,0:T(8,128)S(1)}, f32[136,128]{1,0:T(8,128)S(1)}, u32[]{:S(2)}, u32[]{:S(2)}) collective-permute-start(f32[136,128]{1,0:T(8,128)S(1)} %get-tuple-element.68), channel_id=1, source_target_pairs={{0,32},{32,0},{1,33},{33,1},{2,34},{34,2},{3,35},{35,3},{4,36},{36... | collective-permute-start | bytes 208904 | tf_op jit(solution)/shard_map/ppermute | solution.py:704
  171.3 2.7 %collective-permute-start.3 = (f32[136,128]{1,0:T(8,128)S(1)}, f32[136,128]{1,0:T(8,128)S(1)}, u32[]{:S(2)}, u32[]{:S(2)}) collective-permute-start(f32[136,128]{1,0:T(8,128)S(1)} %get-tuple-element.72), channel_id=1, source_target_pairs={{0,32},{32,0},{1,33},{33,1},{2,34},{34,2},{3,35},{35,3},{4,36},{36... | collective-permute-start | bytes 208904 | tf_op jit(solution)/shard_map/ppermute | solution.py:704
  195.5 2.7 %collective-permute-start.4 = (f32[392,128]{1,0:T(8,128)S(1)}, f32[392,128]{1,0:T(8,128)S(1)}, u32[]{:S(2)}, u32[]{:S(2)}) collective-permute-start(f32[392,128]{1,0:T(8,128)S(1)} %get-tuple-element.77), channel_id=1, source_target_pairs={{0,32},{32,0},{1,33},{33,1},{2,34},{34,2},{3,35},{35,3},{4,36},{36... | collective-permute-start | bytes 602120 | tf_op jit(solution)/shard_map/ppermute | solution.py:704
  219.0 20.2 %all-to-all-start.9 = ((f32[128,5,1,128]{3,2,1,0:T(1,128)}), f32[128,5,1,128]{3,2,1,0:T(1,128)S(1)}, u32[]{:S(2)}, u32[]{:S(2)}) async-start(f32[128,5,1,128]{3,2,1,0:T(1,128)} %bitcast.37), calls=%async_computation.9 | async-start | bytes 655360 | tf_op jit(solution)/shard_map/all_to_all | solution.py:709

commit v3 on v2

--- a/solution.py
+++ b/solution.py
@@ -320,6 +320,15 @@
     return jnp.where(n == 0, first, second).astype(jnp.int32)
 
 
+def weights_kernel(w_ref, f_hi, f_lo, b_hi, b_lo, buf_ref):
+    for l in range(LAYERS):
+        at = pl.ds(l * 3 * C, 3 * C)
+        f_hi[at, :], f_lo[at, :] = split(forward_weights(w_ref, buf_ref, l))
+        if l > 0:
+            at = pl.ds((l - 1) * 3 * C, 3 * C)
+            b_hi[at, :], b_lo[at, :] = split(backward_weights(w_ref, buf_ref, l))
+
+
 def target_lane(cell):
     row = jnp.right_shift(cell, 8)
     col = jnp.bitwise_and(cell, GW - 1)
@@ -340,9 +349,9 @@
 
 
 def first_conv_kernel(
-    g_ref, kept_ref, w_ref,
+    g_ref, kept_ref, wh_ref, wl_ref,
     z_ref, part_ref, ev_hi, ev_lo, od_hi, od_lo,
-    oht_ref, place_ref, buf_ref,
+    oht_ref, place_ref,
 ):
     s = rows_of(g_ref, 2, 0)
     num = rows_of(g_ref, 2, 1)
@@ -357,7 +366,7 @@
     mean_c, inv_c = stats[:C], stats[C:]
     gain, bias = gain_bias(kept_ref, LAYERS)
     lane = lanes128()
-    w_hi, w_lo = split(forward_weights(w_ref, buf_ref, 0))
+    w_hi, w_lo = (ref[pl.ds(0, 3 * C), :] for ref in (wh_ref, wl_ref))
     outer_hi = jnp.concatenate([w_hi[:C], w_hi[2 * C :]], axis=0)
     outer_lo = jnp.concatenate([w_lo[:C], w_lo[2 * C :]], axis=0)
 
@@ -417,7 +426,7 @@
 
 
 def conv_kernel(
-    g_ref, z_ref, gb_ref, w_ref, out_ref, part_ref, stats_ref, s_hi, s_lo, buf_ref, *, layer
+    g_ref, z_ref, gb_ref, wh_ref, wl_ref, out_ref, part_ref, stats_ref, s_hi, s_lo, *, layer
 ):
     stats = columns(gathered_stats(g_ref[...]))
     stats_ref[...] = stats
@@ -425,7 +434,7 @@
     gain, bias = gain_bias(gb_ref, layer - 1)
     lane = lanes128()
     zero_borders((s_hi, s_lo))
-    w_hi, w_lo = split(forward_weights(w_ref, buf_ref, layer))
+    w_hi, w_lo = (ref[pl.ds(layer * 3 * C, 3 * C), :] for ref in (wh_ref, wl_ref))
 
     def activate(at, n, r):
         y = gain * ((z_ref[:, at] - mean) * inv) + bias
@@ -495,7 +504,7 @@
 
 
 def back_kernel(
-    g_ref, z_ref, gy_ref, stats_ref, gb_ref, zp_ref, statsp_ref, w_ref, *refs, layer, stride
+    g_ref, z_ref, gy_ref, stats_ref, gb_ref, zp_ref, statsp_ref, wh_ref, wl_ref, *refs, layer, stride
 ):
     if layer == 1:
         grid0, last3_ref, last2_ref, refs = refs[:4], refs[4], refs[5], refs[6:]
@@ -513,7 +522,7 @@
     gainp, biasp = gain_bias(gb_ref, layer - 1)
     lane = lanes128()
     zero_borders((s_hi, s_lo, a_hi, a_lo))
-    w_hi, w_lo = split(backward_weights(w_ref, buf_ref, layer))
+    w_hi, w_lo = (ref[pl.ds((layer - 1) * 3 * C, 3 * C), :] for ref in (wh_ref, wl_ref))
 
     def turn_back(at, n, r):
         xhat = (z_ref[:, at] - mean) * inv
@@ -742,20 +751,24 @@
         [((C, NS * PILL), F32), tile, ((NS * 4 * MAXP, PILL), F32), ints, ints, ((9, C), F32)] + vectors,
         copies=True,
     )
+    half = [((LAYERS * 3 * C, 3 * C), BF16)] * 2
+    *w_fwd, b_hi, b_lo = call(
+        weights_kernel, "weights", half + [(((LAYERS - 1) * 3 * C, 3 * C), BF16)] * 2, (w,), [buf]
+    )
     got = exchange("pair_p", "pillars", part, peers)
     ev = ((3 * C, NS * POS), BF16)
     od = ((3 * C, NS * (POS + OW)), BF16)
     z, part, *grid0 = call(
         first_conv_kernel, "conv0", [plane, rows8, ev, ev, od, od],
-        (got, kept, w),
-        [((GH * GW, PILL), BF16), ((2 * C, GH * GW), F32), buf],
+        (got, kept, *w_fwd),
+        [((GH * GW, PILL), BF16), ((2 * C, GH * GW), F32)],
     )
     pre = [z]
     stats = []
     for l in range(1, LAYERS):
-        got = exchange("pair_s", "stats", part, peers, part if l == 1 else None)
+        got = exchange("pair_s", "stats", part, peers)
         z, part, st = call(
-            conv_kernel, f"conv{l}", [plane, rows8, tile], (got, pre[-1], kept, w), [pad, pad, buf], layer=l
+            conv_kernel, f"conv{l}", [plane, rows8, tile], (got, pre[-1], kept, *w_fwd), [pad, pad], layer=l
         )
         pre.append(z)
         stats.append(st)
@@ -777,7 +790,7 @@
         gy, sums[l], red, keep, send, *last = call(
             back_kernel, f"back{l}",
             [plane, row, ((blocks, 128), F32), fresh, fresh] + [end] * (l > 1),
-            (got, pre[l], gy, stats[l], kept, pre[l - 1], stats[l - 1], w) + ((*grid0, *ends) if l == 1 else ()),
+            (got, pre[l], gy, stats[l], kept, pre[l - 1], stats[l - 1], b_hi, b_lo) + ((*grid0, *ends) if l == 1 else ()),
             [pad, pad, pad, pad, plane, buf], layer=l, stride=blocks + 1,
         )
         reds.append(red)

time: 246 us -> 245 us (level)
  blocking collectives: 183 us -> 161 us
  starting transfers between devices: 14.7 us -> 26.5 us
  waiting for transfers between devices: 14.9 us -> 23.3 us
    all_to_all x9 -> x8, blocking collectives: 164 us -> 139 us  [to_peers(): return lax.all_to_all(sent, WIDE, 0, 0, tiled=True).reshape(-1, 128)]
    all_to_all x1 -> x2, starting transfers between devices: 6.18 us -> 20 us  [to_peers(): return lax.all_to_all(sent, WIDE, 0, 0, tiled=True).reshape(-1, 128)]
    all_to_all x1 -> x2, waiting for transfers between devices: 10.1 us -> 19.3 us  [to_peers(): return lax.all_to_all(sent, WIDE, 0, 0, tiled=True).reshape(-1, 128)]
    all_gather x4 -> x5, blocking collectives: 13.9 us -> 17.2 us  [exchange(): lax.all_gather(keep, 'k', tiled=True)]
    ppermute x5 -> x4, starting transfers between devices: 8.51 us -> 6.51 us  [partner(): return lax.ppermute(v, 'k', [(0, 1), (1, 0)])]
    pallas_call x21 -> x22, Pallas kernels: 31.2 us -> 32.5 us  [call(): pl.pallas_call(functools.partial(kernel, **params) if params else kernel,...]
  transfers between devices with their start and end apart: 6 -> 6, of which waited for: 6 -> 6; matrix products, arithmetic and copies ran while one was open for 0% -> 0% of each run, Pallas kernels for 2% -> 3%
where the time goes in v3:
time: 245 us; the launch traced here: 244 us
  blocking collectives  161 us (66%)
  Pallas kernels  32.5 us (13%)
  starting transfers between devices  26.5 us (11%)
  waiting for transfers between devices  23.3 us (10%)
    all_to_all x8, blocking collectives, to_peers(): return lax.all_to_all(sent, WIDE, 0, 0, tiled=True).reshape(-1, 128)  139 us
    pallas_call x22, Pallas kernels, call(): pl.pallas_call(functools.partial(kernel, **params) if params else kernel,...  32.5 us
    all_to_all x2, starting transfers between devices, to_peers(): return lax.all_to_all(sent, WIDE, 0, 0, tiled=True).reshape(-1, 128)  20 us
    all_to_all x2, waiting for transfers between devices, to_peers(): return lax.all_to_all(sent, WIDE, 0, 0, tiled=True).reshape(-1, 128)  19.3 us
    all_gather x5, blocking collectives, exchange(): lax.all_gather(keep, 'k', tiled=True)  17.2 us
    ppermute x4, starting transfers between devices, partner(): return lax.ppermute(v, 'k', [(0, 1), (1, 0)])  6.51 us
    all_gather x1, blocking collectives, per_device(): both = lax.all_gather(to_peers(own, peers), 'k', tiled=True)  5.3 us
  transfers between devices with their start and end apart: 6, of which 6 were waited for; matrix products, arithmetic and copies ran while one was open for 0% of the time, Pallas kernels for 3%

profile of v3, /device:TPU:1, one launch (start us, length us, event | category | flops | bytes accessed | tf_op | source)
XLA Modules:
  0.0 244.3 jit_solution(11963763297295636220)
XLA Ops:
  0.6 4.4 %pfn.1 = (f32[80,512]{1,0:T(8,128)}, f32[8,128]{1,0:T(8,128)}) custom-call(f32[256,256]{1,0:T(8,128)} %bitcast.77, s32[2,256]{1,0:T(2,128)} %cnt_in.1, s32[2,256]{1,0:T(2,128)} %cell_in.1, f32[9,64]{1,0:T(8,128)} %w_in.1, f32[4,64]{1,0:T(4,128)} %gain_in.1, f32[4,64]{1,0:T(4,128)} %bias_in.1, f32[1,64]{1,0:T(1,128)} %bitcast.79, f32[1,64]{1,0:T(1,128)} %bitcast.80), custom_call_target="tpu_custom_call" | custom-call | tf_op jit(solution)/shard_map/pfn/pallas_call | solution.py:700
  5.1 4.8 %all_gather.18.refs_0_ = f32[16,128]{1,0:T(8,128)S(1)} all-gather(f32[8,128]{1,0:T(8,128)} %get-tuple-element.50), channel_id=1, replica_groups=mesh['x'=4,'k'=2,'y'=4,'z'=8] {'k'}, dimensions={0}, use_global_device_ids=true | all-gather | bytes 12288 | tf_op jit(solution)/shard_map/all_gather | solution.py:722
  10.6 13.8 %all-to-all-start = ((f32[128,2,1,128]{3,1,2,0:T(2,128)}), f32[128,2,1,128]{3,1,2,0:T(2,128)S(1)}, u32[]{:S(2)}, u32[]{:S(2)}) async-start(f32[128,2,1,128]{3,1,2,0:T(2,128)} %bitcast.4), calls=%async_computation | async-start | bytes 262144 | tf_op jit(solution)/shard_map/all_to_all | solution.py:718
  26.7 9.2 %all-to-all-done = f32[128,2,1,128]{3,1,2,0:T(2,128)S(1)} async-done(((f32[128,2,1,128]{3,1,2,0:T(2,128)}), f32[128,2,1,128]{3,1,2,0:T(2,128)S(1)}, u32[]{:S(2)}, u32[]{:S(2)}) %all-to-all-start) | async-done | bytes 131104 | tf_op jit(solution)/shard_map/all_to_all | solution.py:718
  35.9 2.9 %conv0.1 = (f32[64,1024]{1,0:T(8,128)S(1)}, f32[8,128]{1,0:T(8,128)S(1)}, bf16[192,1024]{1,0:T(8,128)(2,1)S(1)}, bf16[192,1024]{1,0:T(8,128)(2,1)S(1)}, bf16[192...) custom-call(f32[256,128]{1,0:T(8,128)S(1)} %bitcast.62, f32[80,512]{1,0:T(8,128)S(1)} %copy-done, ...), custom_call_target="tpu_custom_call" | custom-call | tf_op jit(solution)/shard_map/conv0/pallas_call | solution.py:700
  38.8 3.2 %all_gather.19.refs_0_ = f32[16,128]{1,0:T(8,128)S(1)} all-gather(f32[8,128]{1,0:T(8,128)S(1)} %get-tuple-element.54), channel_id=1, replica_groups=mesh['x'=4,'k'=2,'y'=4,'z'=8] {'k'}, dimensions={0}, use_global_device_ids=true | all-gather | bytes 12288 | tf_op jit(solution)/shard_map/all_gather | solution.py:722
  42.1 16.1 %all_to_all.50 = f32[128,1,1,128]{3,2,1,0:T(1,128)S(1)} all-to-all(f32[128,1,1,128]{3,2,1,0:T(1,128)S(1)} %bitcast.70), channel_id=1, replica_groups=mesh['x'=4,'k'=2,'y'=4,'z'=8] {'x','y','z'}, dimensions={0} | all-to-all | bytes 131072 | tf_op jit(solution)/shard_map/all_to_all | solution.py:718
  59.6 3.1 %all_gather.20.refs_0_ = f32[16,128]{1,0:T(8,128)S(1)} all-gather(f32[8,128]{1,0:T(8,128)S(1)} %get-tuple-element.56), channel_id=1, replica_groups=mesh['x'=4,'k'=2,'y'=4,'z'=8] {'k'}, dimensions={0}, use_global_device_ids=true | all-gather | bytes 12288 | tf_op jit(solution)/shard_map/all_gather | solution.py:722
  62.8 16.1 %all_to_all.51 = f32[128,1,1,128]{3,2,1,0:T(1,128)S(1)} all-to-all(f32[128,1,1,128]{3,2,1,0:T(1,128)S(1)} %bitcast.71), channel_id=1, replica_groups=mesh['x'=4,'k'=2,'y'=4,'z'=8] {'x','y','z'}, dimensions={0} | all-to-all | bytes 131072 | tf_op jit(solution)/shard_map/all_to_all | solution.py:718
  80.3 3.0 %all_gather.21.refs_0_ = f32[16,128]{1,0:T(8,128)S(1)} all-gather(f32[8,128]{1,0:T(8,128)S(1)} %get-tuple-element.58), channel_id=1, replica_groups=mesh['x'=4,'k'=2,'y'=4,'z'=8] {'k'}, dimensions={0}, use_global_device_ids=true | all-gather | bytes 12288 | tf_op jit(solution)/shard_map/all_gather | solution.py:722
  83.5 16.1 %all_to_all.52 = f32[128,1,1,128]{3,2,1,0:T(1,128)S(1)} all-to-all(f32[128,1,1,128]{3,2,1,0:T(1,128)S(1)} %bitcast.72), channel_id=1, replica_groups=mesh['x'=4,'k'=2,'y'=4,'z'=8] {'x','y','z'}, dimensions={0} | all-to-all | bytes 131072 | tf_op jit(solution)/shard_map/all_to_all | solution.py:718
  101.0 3.0 %all_gather.22.refs_0_ = f32[16,128]{1,0:T(8,128)S(1)} all-gather(f32[8,128]{1,0:T(8,128)S(1)} %get-tuple-element.60), channel_id=1, replica_groups=mesh['x'=4,'k'=2,'y'=4,'z'=8] {'k'}, dimensions={0}, use_global_device_ids=true | all-gather | bytes 12288 | tf_op jit(solution)/shard_map/all_gather | solution.py:722
  104.2 16.1 %all_to_all.53 = f32[128,1,1,128]{3,2,1,0:T(1,128)S(1)} all-to-all(f32[128,1,1,128]{3,2,1,0:T(1,128)S(1)} %bitcast.73), channel_id=1, replica_groups=mesh['x'=4,'k'=2,'y'=4,'z'=8] {'x','y','z'}, dimensions={0} | all-to-all | bytes 131072 | tf_op jit(solution)/shard_map/all_to_all | solution.py:718
  125.3 19.9 %all_to_all.54 = f32[128,4,1,128]{3,1,2,0:T(4,128)S(1)} all-to-all(f32[128,4,1,128]{3,1,2,0:T(4,128)S(1)} %bitcast.58), channel_id=1, replica_groups=mesh['x'=4,'k'=2,'y'=4,'z'=8] {'x','y','z'}, dimensions={0} | all-to-all | bytes 524288 | tf_op jit(solution)/shard_map/all_to_all | solution.py:718
  145.2 2.7 %back3.1 = (f32[64,1024]{1,0:T(8,128)S(1)}, f32[1,128]{1,0:T(1,128)S(1)}, f32[3,128]{1,0:T(4,128)S(1)}, f32[136,128]{1,0:T(8,128)S(1)}, f32[136,128]{1,0:T(8,128)S(1)}, /*index=5*/f32[32,128]{1,0:T(8,128)S(1)}) custom-call(f32[512,128]{1,0:T(8,128)S(1)} %bitcast.60, f32[64,1024]{1,0:T(8,128)S(1)} %get-tuple-element.61.z_ref, ...), custom_call_target="tpu_custom_call" | custom-call | tf_op jit(solution)/shard_map/back3/pallas_call | solution.py:700
  150.6 17.3 %all_to_all.55 = f32[128,2,1,128]{3,1,2,0:T(2,128)S(1)} all-to-all(f32[128,2,1,128]{3,1,2,0:T(2,128)S(1)} %bitcast.64), channel_id=1, replica_groups=mesh['x'=4,'k'=2,'y'=4,'z'=8] {'x','y','z'}, dimensions={0} | all-to-all | bytes 262144 | tf_op jit(solution)/shard_map/all_to_all | solution.py:718
  167.9 2.7 %back2.1 = (f32[64,1024]{1,0:T(8,128)S(1)}, f32[1,128]{1,0:T(1,128)S(1)}, f32[1,128]{1,0:T(1,128)S(1)}, f32[136,128]{1,0:T(8,128)S(1)}, f32[136,128]{1,0:T(8,128)S(1)}, /*index=5*/f32[32,128]{1,0:T(8,128)S(1)}) custom-call(f32[256,128]{1,0:T(8,128)S(1)} %bitcast.63, f32[64,1024]{1,0:T(8,128)S(1)} %get-tuple-element.59.z_ref.zp_ref, ...), custom_call_target="tpu_custom_call" | custom-call | tf_op jit(solution)/shard_map/back2/pallas_call | solution.py:700
  173.1 17.4 %all_to_all.56 = f32[128,2,1,128]{3,1,2,0:T(2,128)S(1)} all-to-all(f32[128,2,1,128]{3,1,2,0:T(2,128)S(1)} %bitcast.65), channel_id=1, replica_groups=mesh['x'=4,'k'=2,'y'=4,'z'=8] {'x','y','z'}, dimensions={0} | all-to-all | bytes 262144 | tf_op jit(solution)/shard_map/all_to_all | solution.py:718
  190.5 3.9 %back1.1 = (f32[64,1024]{1,0:T(8,128)S(1)}, f32[1,128]{1,0:T(1,128)S(1)}, f32[1,128]{1,0:T(1,128)S(1)}, f32[392,128]{1,0:T(8,128)S(1)}, f32[392,128]{1,0:T(8,128)S(1)}) custom-call(f32[256,128]{1,0:T(8,128)S(1)} %bitcast.61, f32[64,1024]{1,0:T(8,128)S(1)} %get-tuple-element.57.z_ref.zp_ref, f32[64,1024]{1,0:T(8,128)S(1)} %get-tuple-element.81.gy_ref, ...), custom_call_target="tpu_custom_call" | custom-call | tf_op jit(solution)/shard_map/back1/pallas_call | solution.py:700
  197.2 19.8 %all_to_all.57 = f32[128,4,1,128]{3,1,2,0:T(4,128)S(1)} all-to-all(f32[128,4,1,128]{3,1,2,0:T(4,128)S(1)} %bitcast.59), channel_id=1, replica_groups=mesh['x'=4,'k'=2,'y'=4,'z'=8] {'x','y','z'}, dimensions={0} | all-to-all | bytes 524288 | tf_op jit(solution)/shard_map/all_to_all | solution.py:718
  217.9 6.2 %all-to-all-start.9 = ((f32[128,5,1,128]{3,2,1,0:T(1,128)}), f32[128,5,1,128]{3,2,1,0:T(1,128)S(1)}, u32[]{:S(2)}, u32[]{:S(2)}) async-start(f32[128,5,1,128]{3,2,1,0:T(1,128)} %bitcast.35), calls=%async_computation.9 | async-start | bytes 655360 | tf_op jit(solution)/shard_map/all_to_all | solution.py:718
  224.1 3.9 %back0.1 = f32[128,256]{1,0:T(8,128)} custom-call(f32[64,1024]{1,0:T(8,128)S(1)} %get-tuple-element.55.z_ref.z0_ref.zp_ref, f32[64,1024]{1,0:T(8,128)S(1)} %get-tuple-element.94.gy_ref, f32[128,128]{1,0:T(8,128)S(1)} %get-tuple-element.62.stats0_ref.statsp_ref.stats_ref, f32[192,128]{1,0:T(8,128)S(1)} %get-tuple-element.95.scale_ref, f32[80,512]{1,0:T(8,128)S(1)} %copy-done, ...), custom_call_target="tpu_custom_call" | custom-call | tf_op jit(solution)/shard_map/back0/pallas_call | solution.py:700
  228.0 10.1 %all-to-all-done.9 = f32[128,5,1,128]{3,2,1,0:T(1,128)S(1)} async-done(((f32[128,5,1,128]{3,2,1,0:T(1,128)}), f32[128,5,1,128]{3,2,1,0:T(1,128)S(1)}, u32[]{:S(2)}, u32[]{:S(2)}) %all-to-all-start.9) | async-done | bytes 327712 | tf_op jit(solution)/shard_map/all_to_all | solution.py:718
  238.1 5.3 %all_gather.23.both_ref = f32[1280,128]{1,0:T(8,128)S(1)} all-gather(f32[640,128]{1,0:T(8,128)S(1)} %bitcast.75), channel_id=1, replica_groups=mesh['x'=4,'k'=2,'y'=4,'z'=8] {'k'}, dimensions={0}, use_global_device_ids=true | all-gather | bytes 983040 | tf_op jit(solution)/shard_map/all_gather | solution.py:804
  (30 shorter events, 22.4 us)
Async XLA Ops:
  0.6 23.8 %copy-start.1 = (f32[4,9,4096]{2,0,1:T(4,128)S(1)}, f32[4,9,4096]{2,0,1:T(4,128)}, u32[]{:S(2)}) copy-start(f32[4,9,4096]{2,0,1:T(4,128)} %param.16) | copy-start | bytes 1769476
  10.6 25.3 %all-to-all-start = ((f32[128,2,1,128]{3,1,2,0:T(2,128)}), f32[128,2,1,128]{3,1,2,0:T(2,128)S(1)}, u32[]{:S(2)}, u32[]{:S(2)}) async-start(f32[128,2,1,128]{3,1,2,0:T(2,128)} %bitcast.4), calls=%async_computation | async-start | bytes 262144 | tf_op jit(solution)/shard_map/all_to_all | solution.py:718
  24.4 11.5 %copy-start = (f32[80,512]{1,0:T(8,128)S(1)}, f32[80,512]{1,0:T(8,128)}, u32[]{:S(2)}) copy-start(f32[80,512]{1,0:T(8,128)} %get-tuple-element.51.kept_ref.gb_ref) | copy-start | bytes 491524
  99.6 20.7 %copy-start.2 = (f32[2,64,4,128]{3,2,1,0:T(4,128)S(1)}, f32[2,64,4,128]{3,2,1,0:T(4,128)}, u32[]{:S(2)}) copy-start(f32[2,64,4,128]{3,2,1,0:T(4,128)} %param.19) | copy-start | bytes 786436
  122.6 2.7 %collective-permute-start = (f32[392,128]{1,0:T(8,128)S(1)}, f32[392,128]{1,0:T(8,128)S(1)}, u32[]{:S(2)}, u32[]{:S(2)}) collective-permute-start(f32[392,128]{1,0:T(8,128)S(1)} %get-tuple-element.69), channel_id=1, source_target_pairs={{0,32},{32,0},{1,33},{33,1},{2,34},{34,2},{3,35},{35,3},{4,36},{36... | collective-permute-start | bytes 602120 | tf_op jit(solution)/shard_map/ppermute | solution.py:713
  147.9 2.7 %collective-permute-start.1 = (f32[136,128]{1,0:T(8,128)S(1)}, f32[136,128]{1,0:T(8,128)S(1)}, u32[]{:S(2)}, u32[]{:S(2)}) collective-permute-start(f32[136,128]{1,0:T(8,128)S(1)} %get-tuple-element.76), channel_id=1, source_target_pairs={{0,32},{32,0},{1,33},{33,1},{2,34},{34,2},{3,35},{35,3},{4,36},{36... | collective-permute-start | bytes 208904 | tf_op jit(solution)/shard_map/ppermute | solution.py:713
  170.6 2.5 %collective-permute-start.2 = (f32[136,128]{1,0:T(8,128)S(1)}, f32[136,128]{1,0:T(8,128)S(1)}, u32[]{:S(2)}, u32[]{:S(2)}) collective-permute-start(f32[136,128]{1,0:T(8,128)S(1)} %get-tuple-element.80), channel_id=1, source_target_pairs={{0,32},{32,0},{1,33},{33,1},{2,34},{34,2},{3,35},{35,3},{4,36},{36... | collective-permute-start | bytes 208904 | tf_op jit(solution)/shard_map/ppermute | solution.py:713
  194.4 2.7 %collective-permute-start.3 = (f32[392,128]{1,0:T(8,128)S(1)}, f32[392,128]{1,0:T(8,128)S(1)}, u32[]{:S(2)}, u32[]{:S(2)}) collective-permute-start(f32[392,128]{1,0:T(8,128)S(1)} %get-tuple-element.85), channel_id=1, source_target_pairs={{0,32},{32,0},{1,33},{33,1},{2,34},{34,2},{3,35},{35,3},{4,36},{36... | collective-permute-start | bytes 602120 | tf_op jit(solution)/shard_map/ppermute | solution.py:713
  217.9 20.2 %all-to-all-start.9 = ((f32[128,5,1,128]{3,2,1,0:T(1,128)}), f32[128,5,1,128]{3,2,1,0:T(1,128)S(1)}, u32[]{:S(2)}, u32[]{:S(2)}) async-start(f32[128,5,1,128]{3,2,1,0:T(1,128)} %bitcast.35), calls=%async_computation.9 | async-start | bytes 655360 | tf_op jit(solution)/shard_map/all_to_all | solution.py:718
